TPU v7x, 128 devices: a whole 4x4x4 slice. The times are simulated.
128 devices in a mesh: gx: 4 (over x), gy: 32 (over z, y, core).
Axes of the slice: x: 4, y: 4, z: 4, core: 2. Of those that a mesh axis runs over, the one named last changes fastest.
Arguments:
- source_values: bfloat16 [16384, 64, 128], P(('gx', 'gy')), may hold values from -6 to 6
- leaf_maps: bfloat16 [16384, 32, 128], P(('gx', 'gy')), may hold values from -0.5 to 0.5
- source_transfers: bfloat16 [4, 16384, 32, 128], P(None, ('gx', 'gy')), may hold values from -0.5 to 0.5
- target_transfers: bfloat16 [4, 16384, 32, 128], P(None, ('gx', 'gy')), may hold values from -0.5 to 0.5
Outputs:
- target_coeffs: bfloat16 [16384, 32, 128], P(('gx', 'gy'))
All inputs are finite; a program needn't handle non-finite values.
Results may differ from a plain program's by a relative error of at most 0.012.
Values may be sent and summed in bfloat16 or wider, within the bound.
A program may use at most 128 MiB of HBM per device.

v0:
```python
import jax
import jax.numpy as jnp
from jax import lax
from jax.sharding import PartitionSpec as P

RHS = 64


def swapped(block, axis, apart):
    count = lax.axis_size(axis)
    route = []
    for low in range(count):
        high = low | 1 << apart
        if high != low and high < count:
            route += [(low, high), (high, low)]
    return lax.ppermute(block, axis, route)


def rotated(block):
    nboxes, rows_n, cols = block.shape
    parts = block.reshape(nboxes, rows_n, cols // (2 * RHS), 2, RHS)
    turned = jnp.concatenate([-parts[:, :, :, 1:], parts[:, :, :, :1]], axis=3)
    return turned.reshape(block.shape)


def complex_apply(matrix, operand):
    return jnp.einsum("bik,bkc->bic", matrix, operand, preferred_element_type=jnp.float32).astype(
        jnp.bfloat16
    )


def mix_pair(coeffs, partner, transfer):
    operand = jnp.concatenate([coeffs, rotated(coeffs), partner, rotated(partner)], axis=1)
    return complex_apply(transfer, operand)


def apply_level(coeffs, transfer, device_bit, low_bits):
    if device_bit < low_bits:
        partner = swapped(coeffs, "gy", device_bit)
    else:
        partner = swapped(coeffs, "gx", device_bit - low_bits)
    return mix_pair(coeffs, partner, transfer)


def local(source_values, leaf_maps, source_transfers, target_transfers):
    leaf_operand = jnp.concatenate([source_values, rotated(source_values)], axis=1)
    coeffs = complex_apply(leaf_maps, leaf_operand)
    low_bits = lax.axis_size("gy").bit_length() - 1
    all_bits = low_bits + lax.axis_size("gx").bit_length() - 1
    levels = source_transfers.shape[0]
    for level_no in range(levels):
        coeffs = apply_level(coeffs, source_transfers[level_no], level_no % all_bits, low_bits)
    coeffs = lax.all_to_all(coeffs, ("gx", "gy"), split_axis=0, concat_axis=0, tiled=True)
    for level_no in range(levels):
        coeffs = apply_level(
            coeffs, target_transfers[level_no], (all_bits - 1 - level_no) % all_bits, low_bits
        )
    return coeffs


def solution(mesh):
    return jax.shard_map(
        local,
        mesh=mesh,
        in_specs=(
            P(("gx", "gy"), None, None),
            P(("gx", "gy"), None, None),
            P(None, ("gx", "gy"), None, None),
            P(None, ("gx", "gy"), None, None),
        ),
        out_specs=P(("gx", "gy"), None, None),
        check_vma=False,
    )
```

profile of v0, /device:TPU:4, one launch (start us, length us, event | category | flops | bytes accessed | tf_op | source)
XLA Modules:
  0.0 269.7 jit_solution(5166075585074353720)
XLA Ops:
  0.0 3.4 %copy.5 = bf16[128,64,128]{0,2,1:T(8,128)(2,1)S(1)} copy(bf16[128,64,128]{2,1,0:T(8,128)(2,1)} %param.4) | data formatting | bytes 4194304 | tf_op args[0]
  3.8 2.9 %copy.6 = bf16[128,64,128]{2,1,0:T(8,128)(2,1)} copy(bf16[128,64,128]{0,2,1:T(8,128)(2,1)S(1)} %bitcast.78) | data formatting | bytes 4194304 | tf_op jit(solution)/shard_map/reshape | solution.py:23
  6.7 3.4 %fusion.95 = bf16[128,32,128]{2,1,0:T(8,128)(2,1)S(1)} fusion(bf16[128,32,128]{2,1,0:T(8,128)(2,1)S(1)} %copy-done, bf16[128,64,128]{2,1,0:T(8,128)(2,1)} %copy.6, bf16[128,64,128]{2,1,0:T(8,128)(2,1)} %param.4), kind=kOutput, calls=%fused_computation.78 | convolution fusion | flops 143130624 | bytes 6291456 | tf_op jit(solution)/shard_map/bik,bkc->bic/dot_general | solution.py:27
  10.2 1.0 copy.7
  11.4 1.7 copy.9
  13.1 1.9 copy.8
  15.3 1.7 copy.10
  17.0 3.4 %fusion.98 = bf16[128,32,128]{2,1,0:T(8,128)(2,1)S(1)} fusion(bf16[128,32,128]{2,1,0:T(8,128)(2,1)} %copy.10, bf16[128,32,128]{2,1,0:T(8,128)(2,1)} %collective-permute-done, bf16[128,32,128]{2,1,0:T(8,128)(2,1)} %copy.9, bf16[128,32,128]{2,1,0:T(8,128)(2,1)S(1)} %fusion.95, bf16[4,128,32,128]{3,2,1,0:T(8,128)(2,1)} %param.6), kind=kOutput, calls=%fused_computation.79 | convolution fusion | flops 151519232 | bytes 6291456 | tf_op jit(solution)/shard_map/bik,bkc->bic/dot_general | solution.py:27
  20.3 1.7 collective-permute-start.1
  23.2 1.7 copy.13
  24.9 21.1 %collective-permute-done.1 = bf16[128,32,128]{2,1,0:T(8,128)(2,1)S(1)} collective-permute-done((bf16[128,32,128]{2,1,0:T(8,128)(2,1)S(1)}, bf16[128,32,128]{2,1,0:T(8,128)(2,1)S(1)}, u32[]{:S(2)}, u32[]{:S(2)}) %collective-permute-start.1) | collective-permute-done | bytes 1048608 | tf_op jit(solution)/shard_map/ppermute | solution.py:16
  46.0 1.0 copy.12
  47.2 1.7 copy.14
  48.8 3.0 %fusion.101 = bf16[128,32,128]{2,1,0:T(8,128)(2,1)S(1)} fusion(bf16[128,32,128]{2,1,0:T(8,128)(2,1)} %copy.14, bf16[128,32,128]{2,1,0:T(8,128)(2,1)S(1)} %collective-permute-done.1, bf16[128,32,128]{2,1,0:T(8,128)(2,1)} %copy.13, bf16[128,32,128]{2,1,0:T(8,128)(2,1)S(1)} %fusion.98, bf16[4,128,32,128]{3,2,1,0:T(8,128)(2,1)} %param.6), kind=kOutput, calls=%fused_computation.80 | convolution fusion | flops 151519232 | bytes 6291456 | tf_op jit(solution)/shard_map/bik,bkc->bic/dot_general | solution.py:27
  51.9 3.5 %collective-permute-start.2 = (bf16[128,32,128]{2,1,0:T(8,128)(2,1)S(1)}, bf16[128,32,128]{2,1,0:T(8,128)(2,1)}, u32[]{:S(2)}, u32[]{:S(2)}) collective-permute-start(bf16[128,32,128]{2,1,0:T(8,128)(2,1)S(1)} %fusion.101), channel_id=1, source_target_pairs={{0,4},{4,0},{1,5},{5,1},{2,6},{6,2},{3,7},{7,3},{8,12},{12,8},{9,1... | collective-permute-start | bytes 3145736 | tf_op jit(solution)/shard_map/ppermute | solution.py:16
  56.5 1.7 copy.17
  58.2 20.2 %collective-permute-done.2 = bf16[128,32,128]{2,1,0:T(8,128)(2,1)} collective-permute-done((bf16[128,32,128]{2,1,0:T(8,128)(2,1)S(1)}, bf16[128,32,128]{2,1,0:T(8,128)(2,1)}, u32[]{:S(2)}, u32[]{:S(2)}) %collective-permute-start.2) | collective-permute-done | bytes 1048608 | tf_op jit(solution)/shard_map/ppermute | solution.py:16
  78.4 1.9 copy.16
  80.6 1.7 copy.18
  82.3 3.4 %fusion.104 = bf16[128,32,128]{2,1,0:T(8,128)(2,1)S(1)} fusion(bf16[128,32,128]{2,1,0:T(8,128)(2,1)} %copy.18, bf16[128,32,128]{2,1,0:T(8,128)(2,1)} %collective-permute-done.2, bf16[128,32,128]{2,1,0:T(8,128)(2,1)} %copy.17, bf16[128,32,128]{2,1,0:T(8,128)(2,1)S(1)} %fusion.101, bf16[4,128,32,128]{3,2,1,0:T(8,128)(2,1)} %param.6), kind=kOutput, calls=%fused_computation.81 | convolution fusion | flops 151519232 | bytes 6291456 | tf_op jit(solution)/shard_map/bik,bkc->bic/dot_general | solution.py:27
  85.6 2.0 collective-permute-start.3
  88.8 1.7 copy.21
  90.5 19.2 %collective-permute-done.3 = bf16[128,32,128]{2,1,0:T(8,128)(2,1)S(1)} collective-permute-done((bf16[128,32,128]{2,1,0:T(8,128)(2,1)S(1)}, bf16[128,32,128]{2,1,0:T(8,128)(2,1)S(1)}, u32[]{:S(2)}, u32[]{:S(2)}) %collective-permute-start.3) | collective-permute-done | bytes 1048608 | tf_op jit(solution)/shard_map/ppermute | solution.py:16
  110.9 1.7 copy.22
  112.6 3.0 %fusion.107 = bf16[128,32,128]{2,1,0:T(8,128)(2,1)S(1)} fusion(bf16[128,32,128]{2,1,0:T(8,128)(2,1)} %copy.22, bf16[128,32,128]{2,1,0:T(8,128)(2,1)S(1)} %collective-permute-done.3, bf16[128,32,128]{2,1,0:T(8,128)(2,1)} %copy.21, bf16[128,32,128]{2,1,0:T(8,128)(2,1)S(1)} %fusion.104, bf16[4,128,32,128]{3,2,1,0:T(8,128)(2,1)} %param.6), kind=kOutput, calls=%fused_computation.82 | convolution fusion | flops 151519232 | bytes 6291456 | tf_op jit(solution)/shard_map/bik,bkc->bic/dot_general | solution.py:27
  115.6 27.6 %all_to_all.5 = bf16[128,32,128]{2,1,0:T(8,128)(2,1)S(1)} all-to-all(bf16[128,32,128]{2,1,0:T(8,128)(2,1)S(1)} %fusion.107), channel_id=1, replica_groups=mesh['gx'=4,'gy'=32] {'gx','gy'}, dimensions={0} | all-to-all | bytes 2097152 | tf_op jit(solution)/shard_map/all_to_all | solution.py:53
  143.2 2.8 %collective-permute-start.4 = (bf16[128,32,128]{2,1,0:T(8,128)(2,1)S(1)}, bf16[128,32,128]{2,1,0:T(8,128)(2,1)S(1)}, u32[]{:S(2)}, u32[]{:S(2)}) collective-permute-start(bf16[128,32,128]{2,1,0:T(8,128)(2,1)S(1)} %all_to_all.5), channel_id=1, source_target_pairs={{0,64},{64,0},{32,96},{96,32},{1,65},{65,1},{33,97},{97,33},{2,66}... | collective-permute-start | bytes 3145736 | tf_op jit(solution)/shard_map/ppermute | solution.py:16
  147.2 1.7 copy.25
  148.9 21.0 %collective-permute-done.4 = bf16[128,32,128]{2,1,0:T(8,128)(2,1)S(1)} collective-permute-done((bf16[128,32,128]{2,1,0:T(8,128)(2,1)S(1)}, bf16[128,32,128]{2,1,0:T(8,128)(2,1)S(1)}, u32[]{:S(2)}, u32[]{:S(2)}) %collective-permute-start.4) | collective-permute-done | bytes 1048608 | tf_op jit(solution)/shard_map/ppermute | solution.py:16
  171.1 1.7 copy.26
  172.8 3.0 %fusion.110 = bf16[128,32,128]{2,1,0:T(8,128)(2,1)S(1)} fusion(bf16[128,32,128]{2,1,0:T(8,128)(2,1)} %copy.26, bf16[128,32,128]{2,1,0:T(8,128)(2,1)S(1)} %collective-permute-done.4, bf16[128,32,128]{2,1,0:T(8,128)(2,1)} %copy.25, bf16[128,32,128]{2,1,0:T(8,128)(2,1)S(1)} %all_to_all.5, bf16[4,128,32,128]{3,2,1,0:T(8,128)(2,1)} %param.7), kind=kOutput, calls=%fused_computation.83 | convolution fusion | flops 151519232 | bytes 6291456 | tf_op jit(solution)/shard_map/bik,bkc->bic/dot_general | solution.py:27
  175.8 1.4 collective-permute-start.5
  178.4 1.7 copy.29
  180.1 20.4 %collective-permute-done.5 = bf16[128,32,128]{2,1,0:T(8,128)(2,1)} collective-permute-done((bf16[128,32,128]{2,1,0:T(8,128)(2,1)S(1)}, bf16[128,32,128]{2,1,0:T(8,128)(2,1)}, u32[]{:S(2)}, u32[]{:S(2)}) %collective-permute-start.5) | collective-permute-done | bytes 1048608 | tf_op jit(solution)/shard_map/ppermute | solution.py:16
  200.5 1.9 copy.28
  202.6 1.7 copy.30
  204.3 3.4 %fusion.113 = bf16[128,32,128]{2,1,0:T(8,128)(2,1)S(1)} fusion(bf16[128,32,128]{2,1,0:T(8,128)(2,1)} %copy.30, bf16[128,32,128]{2,1,0:T(8,128)(2,1)} %collective-permute-done.5, bf16[128,32,128]{2,1,0:T(8,128)(2,1)} %copy.29, bf16[128,32,128]{2,1,0:T(8,128)(2,1)S(1)} %fusion.110, bf16[4,128,32,128]{3,2,1,0:T(8,128)(2,1)} %param.7), kind=kOutput, calls=%fused_computation.84 | convolution fusion | flops 151519232 | bytes 6291456 | tf_op jit(solution)/shard_map/bik,bkc->bic/dot_general | solution.py:27
  207.7 1.3 collective-permute-start.6
  210.2 1.7 copy.33
  211.9 20.8 %collective-permute-done.6 = bf16[128,32,128]{2,1,0:T(8,128)(2,1)S(1)} collective-permute-done((bf16[128,32,128]{2,1,0:T(8,128)(2,1)S(1)}, bf16[128,32,128]{2,1,0:T(8,128)(2,1)S(1)}, u32[]{:S(2)}, u32[]{:S(2)}) %collective-permute-start.6) | collective-permute-done | bytes 1048608 | tf_op jit(solution)/shard_map/ppermute | solution.py:16
  233.9 1.7 copy.34
  235.6 3.0 %fusion.116 = bf16[128,32,128]{2,1,0:T(8,128)(2,1)S(1)} fusion(bf16[128,32,128]{2,1,0:T(8,128)(2,1)} %copy.34, bf16[128,32,128]{2,1,0:T(8,128)(2,1)S(1)} %collective-permute-done.6, bf16[128,32,128]{2,1,0:T(8,128)(2,1)} %copy.33, bf16[128,32,128]{2,1,0:T(8,128)(2,1)S(1)} %fusion.113, bf16[4,128,32,128]{3,2,1,0:T(8,128)(2,1)} %param.7), kind=kOutput, calls=%fused_computation.85 | convolution fusion | flops 151519232 | bytes 6291456 | tf_op jit(solution)/shard_map/bik,bkc->bic/dot_general | solution.py:27
  238.7 1.0 copy.35
  239.9 1.7 copy.37
  241.6 19.7 %collective-permute-done.7 = bf16[128,32,128]{2,1,0:T(8,128)(2,1)} collective-permute-done((bf16[128,32,128]{2,1,0:T(8,128)(2,1)S(1)}, bf16[128,32,128]{2,1,0:T(8,128)(2,1)}, u32[]{:S(2)}, u32[]{:S(2)}) %collective-permute-start.7) | collective-permute-done | bytes 1048608 | tf_op jit(solution)/shard_map/ppermute | solution.py:16
  261.4 2.0 copy.36
  263.6 1.7 copy.38
  265.4 4.4 %fusion.119 = bf16[128,32,128]{2,1,0:T(8,128)(2,1)} fusion(bf16[128,32,128]{2,1,0:T(8,128)(2,1)} %copy.38, bf16[128,32,128]{2,1,0:T(8,128)(2,1)} %collective-permute-done.7, bf16[128,32,128]{2,1,0:T(8,128)(2,1)} %copy.37, bf16[128,32,128]{2,1,0:T(8,128)(2,1)S(1)} %copy-done.3, bf16[4,128,32,128]{3,2,1,0:T(8,128)(2,1)} %param.7), kind=kOutput, calls=%fused_computation.86 | convolution fusion | flops 151519232 | bytes 6291456 | tf_op jit(solution)/shard_map/bik,bkc->bic/dot_general | solution.py:27
  (54 shorter events, 12.6 us)
Async XLA Ops:
  0.0 6.7 %copy-start = (bf16[128,32,128]{2,1,0:T(8,128)(2,1)S(1)}, bf16[128,32,128]{2,1,0:T(8,128)(2,1)}, u32[]{:S(2)}) copy-start(bf16[128,32,128]{2,1,0:T(8,128)(2,1)} %param.5) | copy-start | bytes 3145732
  10.1 3.0 %collective-permute-start = (bf16[128,32,128]{2,1,0:T(8,128)(2,1)S(1)}, bf16[128,32,128]{2,1,0:T(8,128)(2,1)}, u32[]{:S(2)}, u32[]{:S(2)}) collective-permute-start(bf16[128,32,128]{2,1,0:T(8,128)(2,1)S(1)} %fusion.95), channel_id=1, source_target_pairs={{0,1},{1,0},{2,3},{3,2},{4,5},{5,4},{6,7},{7,6},{8,9},{9,8},{10,11... | collective-permute-start | bytes 3145736 | tf_op jit(solution)/shard_map/ppermute | solution.py:16
  20.3 25.6 %collective-permute-start.1 = (bf16[128,32,128]{2,1,0:T(8,128)(2,1)S(1)}, bf16[128,32,128]{2,1,0:T(8,128)(2,1)S(1)}, u32[]{:S(2)}, u32[]{:S(2)}) collective-permute-start(bf16[128,32,128]{2,1,0:T(8,128)(2,1)S(1)} %fusion.98), channel_id=1, source_target_pairs={{0,2},{2,0},{1,3},{3,1},{4,6},{6,4},{5,7},{7,5},{8,10},{10,8},{9,1... | collective-permute-start | bytes 3145736 | tf_op jit(solution)/shard_map/ppermute | solution.py:16
  51.9 26.6 %collective-permute-start.2 = (bf16[128,32,128]{2,1,0:T(8,128)(2,1)S(1)}, bf16[128,32,128]{2,1,0:T(8,128)(2,1)}, u32[]{:S(2)}, u32[]{:S(2)}) collective-permute-start(bf16[128,32,128]{2,1,0:T(8,128)(2,1)S(1)} %fusion.101), channel_id=1, source_target_pairs={{0,4},{4,0},{1,5},{5,1},{2,6},{6,2},{3,7},{7,3},{8,12},{12,8},{9,1... | collective-permute-start | bytes 3145736 | tf_op jit(solution)/shard_map/ppermute | solution.py:16
  85.6 24.1 %collective-permute-start.3 = (bf16[128,32,128]{2,1,0:T(8,128)(2,1)S(1)}, bf16[128,32,128]{2,1,0:T(8,128)(2,1)S(1)}, u32[]{:S(2)}, u32[]{:S(2)}) collective-permute-start(bf16[128,32,128]{2,1,0:T(8,128)(2,1)S(1)} %fusion.104), channel_id=1, source_target_pairs={{0,8},{8,0},{1,9},{9,1},{2,10},{10,2},{3,11},{11,3},{4,12},{12,4},... | collective-permute-start | bytes 3145736 | tf_op jit(solution)/shard_map/ppermute | solution.py:16
  143.2 26.6 %collective-permute-start.4 = (bf16[128,32,128]{2,1,0:T(8,128)(2,1)S(1)}, bf16[128,32,128]{2,1,0:T(8,128)(2,1)S(1)}, u32[]{:S(2)}, u32[]{:S(2)}) collective-permute-start(bf16[128,32,128]{2,1,0:T(8,128)(2,1)S(1)} %all_to_all.5), channel_id=1, source_target_pairs={{0,64},{64,0},{32,96},{96,32},{1,65},{65,1},{33,97},{97,33},{2,66}... | collective-permute-start | bytes 3145736 | tf_op jit(solution)/shard_map/ppermute | solution.py:16
  175.8 24.7 %collective-permute-start.5 = (bf16[128,32,128]{2,1,0:T(8,128)(2,1)S(1)}, bf16[128,32,128]{2,1,0:T(8,128)(2,1)}, u32[]{:S(2)}, u32[]{:S(2)}) collective-permute-start(bf16[128,32,128]{2,1,0:T(8,128)(2,1)S(1)} %fusion.110), channel_id=1, source_target_pairs={{0,32},{32,0},{64,96},{96,64},{1,33},{33,1},{65,97},{97,65},{2,34}... | collective-permute-start | bytes 3145736 | tf_op jit(solution)/shard_map/ppermute | solution.py:16
  207.7 25.0 %collective-permute-start.6 = (bf16[128,32,128]{2,1,0:T(8,128)(2,1)S(1)}, bf16[128,32,128]{2,1,0:T(8,128)(2,1)S(1)}, u32[]{:S(2)}, u32[]{:S(2)}) collective-permute-start(bf16[128,32,128]{2,1,0:T(8,128)(2,1)S(1)} %fusion.113), channel_id=1, source_target_pairs={{0,16},{16,0},{1,17},{17,1},{2,18},{18,2},{3,19},{19,3},{4,20},{20... | collective-permute-start | bytes 3145736 | tf_op jit(solution)/shard_map/ppermute | solution.py:16
  238.6 3.0 %copy-start.2 = (bf16[128,32,128]{2,1,0:T(8,128)(2,1)}, bf16[128,32,128]{2,1,0:T(8,128)(2,1)S(1)}, u32[]{:S(2)}) copy-start(bf16[128,32,128]{2,1,0:T(8,128)(2,1)S(1)} %fusion.116) | copy-start | bytes 3145732
  238.6 22.8 %collective-permute-start.7 = (bf16[128,32,128]{2,1,0:T(8,128)(2,1)S(1)}, bf16[128,32,128]{2,1,0:T(8,128)(2,1)}, u32[]{:S(2)}, u32[]{:S(2)}) collective-permute-start(bf16[128,32,128]{2,1,0:T(8,128)(2,1)S(1)} %fusion.116), channel_id=1, source_target_pairs={{0,8},{8,0},{1,9},{9,1},{2,10},{10,2},{3,11},{11,3},{4,12},{12,4},... | collective-permute-start | bytes 3145736 | tf_op jit(solution)/shard_map/ppermute | solution.py:16
  261.4 4.0 %copy-start.3 = (bf16[128,32,128]{2,1,0:T(8,128)(2,1)S(1)}, bf16[128,32,128]{2,1,0:T(8,128)(2,1)}, u32[]{:S(2)}) copy-start(bf16[128,32,128]{2,1,0:T(8,128)(2,1)} %copy-done.2) | copy-start | bytes 3145732
  263.6 6.1 %copy-start.1 = (bf16[128,32,128]{2,1,0:T(8,128)(2,1)S(1)}, bf16[128,32,128]{2,1,0:T(8,128)(2,1)}, u32[]{:S(2)}) copy-start(bf16[128,32,128]{2,1,0:T(8,128)(2,1)} %param.5) | copy-start | bytes 3145732
where the time goes:
time: 270 us
  waiting for transfers between devices  142 us (53%)
  local copies, waits for them, and re-layouts  52.9 us (20%)
  matrix products  30 us (11%)
  blocking collectives  27.6 us (10%)
  starting transfers between devices  12.8 us (5%)
  other arithmetic  3.65 us (1%)
    ppermute x8, waiting for transfers between devices, swapped(): return lax.ppermute(block, axis, route)  142 us
    reshape x17, local copies, waits for them, and re-layouts, rotated(): return turned.reshape(block.shape)  30 us
    dot_general x9, matrix products, complex_apply(): jnp.einsum('bik,bkc->bic', matrix, operand, preferred_element_type=jnp.fl...  30 us
    all_to_all x1, blocking collectives, local(): lax.all_to_all(coeffs, ('gx', 'gy'), split_axis=0, concat_axis=0, tiled=T...  27.6 us
    ppermute x8, starting transfers between devices, swapped(): return lax.ppermute(block, axis, route)  12.8 us
    ppermute x8, local copies, waits for them, and re-layouts, swapped(): return lax.ppermute(block, axis, route)  11.7 us
    convert_element_type x7, local copies, waits for them, and re-layouts, complex_apply(): jnp.einsum('bik,bkc->bic', matrix, operand, preferred_element_type=jnp.fl...  6.81 us
  transfers between devices with their start and end apart: 8, of which 7 were waited for; matrix products, arithmetic and copies ran while one was open for 9% of the time, Pallas kernels for 0%

commit v1 on v0

v1 whole, which is shorter than its diff:
```python
import functools

import jax
import jax.numpy as jnp
from jax import lax
from jax.experimental import pallas as pl
from jax.experimental.pallas import tpu as pltpu
from jax.sharding import PartitionSpec as P

MESH = pl.DeviceIdType.MESH
BF16 = jnp.bfloat16
F32 = jnp.float32


def turned(x):
    wide = pltpu.roll(x.astype(F32), 64, x.ndim - 1)
    lane = lax.broadcasted_iota(jnp.int32, wide.shape, wide.ndim - 1)
    return jnp.where(lane < 64, -wide, wide).astype(BF16)


def dot(a, b):
    return jnp.dot(a, b, preferred_element_type=F32).astype(BF16)


def mixed(own, partner, transfer):
    operand = jnp.concatenate([own, turned(own), partner, turned(partner)], axis=0)
    return dot(transfer, operand)


def mixed_pair(a, b, transfer_a, transfer_b):
    ta, tb = turned(a), turned(b)
    out_a = dot(transfer_a, jnp.concatenate([a, ta, b, tb], axis=0))
    out_b = dot(transfer_b, jnp.concatenate([b, tb, a, ta], axis=0))
    return out_a, out_b


def kernel(
    src, leaf, st, tt, out,
    src_v, leaf_v, s0, sb, tb, c0, c0p, c1, cb, ya, yb, zp, wa, wb,
    load_sem, own_sem, s_send, s_recv, t_send, t_recv, p_send, p_recv,
    y_send, y_recv, z_send, z_recv, r_send, r_recv,
):
    x = lax.axis_index("gx")
    g = lax.axis_index("gy")
    z = g // 8
    yc = g % 8
    core = g % 2
    xz = x * 4 + z

    def at_xz(i, j):
        to_x, to_z = (x + i) % 4, (z + j) % 4
        return (to_x, to_z * 8 + yc), to_x * 4 + to_z

    def at_yc(r):
        to = (yc + r) % 8
        return (x, z * 8 + to), to

    xz_offsets = [(i, j) for i in range(4) for j in range(4) if (i, j) != (0, 0)]
    yc_offsets = list(range(1, 8))
    core_mate = (x, g + 1 - 2 * core)
    z_mate = (x, (z + 1 - 2 * (z % 2)) * 8 + yc)

    loads = [
        pltpu.make_async_copy(src, src_v, load_sem.at[0]),
        pltpu.make_async_copy(leaf, leaf_v, load_sem.at[1]),
        pltpu.make_async_copy(st.at[0], s0, load_sem.at[2]),
    ]
    for copy in loads:
        copy.start()
    own_copies = [pltpu.make_async_copy(tt.at[:, xz], tb.at[:, xz], own_sem.at[3])]
    for level in range(3):
        own_copies.append(
            pltpu.make_async_copy(st.at[level + 1, :, yc], sb.at[level, yc], own_sem.at[level])
        )

    barrier = pltpu.get_barrier_semaphore()
    for i, j in xz_offsets:
        pl.semaphore_signal(barrier, inc=1, device_id=at_xz(i, j)[0], device_id_type=MESH)
    for r in yc_offsets:
        pl.semaphore_signal(barrier, inc=1, device_id=at_yc(r)[0], device_id_type=MESH)
    pl.semaphore_wait(barrier, len(xz_offsets) + len(yc_offsets))

    def s_copy(level, r):
        device, to = at_yc(r)
        return pltpu.make_async_remote_copy(
            src_ref=st.at[level + 1, :, to],
            dst_ref=sb.at[level, yc],
            send_sem=s_send.at[level, r],
            recv_sem=s_recv.at[level, r],
            device_id=device,
            device_id_type=MESH,
        )

    def t_copy(k):
        device, to = at_xz(*xz_offsets[k])
        return pltpu.make_async_remote_copy(
            src_ref=tt.at[:, to],
            dst_ref=tb.at[:, xz],
            send_sem=t_send.at[k],
            recv_sem=t_recv.at[k],
            device_id=device,
            device_id_type=MESH,
        )

    for r in yc_offsets:
        s_copy(0, r).start()
    for k in range(15):
        t_copy(k).start()
    for copy in own_copies:
        copy.start()

    def p_copy(q):
        return pltpu.make_async_remote_copy(
            src_ref=c0.at[pl.ds(4 * q, 4)],
            dst_ref=c0p.at[pl.ds(4 * q, 4)],
            send_sem=p_send.at[q],
            recv_sem=p_recv.at[q],
            device_id=core_mate,
            device_id_type=MESH,
        )

    loads[0].wait()
    loads[1].wait()
    for q in range(4):
        def leaf_body(n, carry, q=q):
            a = 4 * q + n
            for b in range(8):
                v = src_v[a, b]
                c0[a, b] = dot(leaf_v[a, b], jnp.concatenate([v, turned(v)], axis=0))
            return carry

        lax.fori_loop(0, 4, leaf_body, 0)
        p_copy(q).start()

    def y_copy(q, r):
        device, to = at_yc(r)
        return pltpu.make_async_remote_copy(
            src_ref=c1.at[to, pl.ds(4 * q, 4)],
            dst_ref=cb.at[yc, pl.ds(4 * q, 4)],
            send_sem=y_send.at[q, r],
            recv_sem=y_recv.at[q, r],
            device_id=device,
            device_id_type=MESH,
        )

    loads[2].wait()
    for q in range(4):
        p_copy(q).wait_recv()

        def first_body(n, carry, q=q):
            a = 4 * q + n
            for b in range(8):
                c1[b, a] = mixed(c0[a, b], c0p[a, b], s0[a, b])
            return carry

        lax.fori_loop(0, 4, first_body, 0)
        for r in yc_offsets:
            y_copy(q, r).start()
    for level in (1, 2):
        for r in yc_offsets:
            s_copy(level, r).start()
    cb[yc] = c1[yc]

    def y_level(q, bit, level, source, target):
        def body(n, carry):
            a = 4 * q + n
            for b in range(8):
                if b & bit == 0:
                    out_a, out_b = mixed_pair(
                        source[b, a], source[b | bit, a], sb[level, b, a], sb[level, b | bit, a]
                    )
                    target[b, a] = out_a
                    target[b | bit, a] = out_b
            return carry

        lax.fori_loop(0, 4, body, 0)

    for r in yc_offsets:
        s_copy(0, r).wait_recv()
    own_copies[1].wait()
    for q in range(4):
        for r in yc_offsets:
            y_copy(q, r).wait_recv()
        y_level(q, 2, 0, cb, ya)
    for r in yc_offsets:
        s_copy(1, r).wait_recv()
    own_copies[2].wait()
    for q in range(4):
        y_level(q, 4, 1, ya, yb)

    def z_copy(q):
        return pltpu.make_async_remote_copy(
            src_ref=yb.at[pl.ds(2 * q, 2)],
            dst_ref=zp.at[pl.ds(2 * q, 2)],
            send_sem=z_send.at[q],
            recv_sem=z_recv.at[q],
            device_id=z_mate,
            device_id_type=MESH,
        )

    for q in range(4):
        z_copy(q).start()
    for r in yc_offsets:
        s_copy(2, r).wait_recv()
    own_copies[3].wait()
    for k in range(15):
        t_copy(k).wait_recv()
    own_copies[0].wait()

    def r_copy(q, k):
        device, to = at_xz(*xz_offsets[k])
        return pltpu.make_async_remote_copy(
            src_ref=wa.at[pl.ds(2 * q, 2), to],
            dst_ref=out.at[xz, pl.ds(2 * q, 2)],
            send_sem=r_send.at[q, k],
            recv_sem=r_recv.at[q, k],
            device_id=device,
            device_id_type=MESH,
        )

    def last_body(q, carry):
        z_copy(q).wait_recv()
        for h in range(2):
            b = 2 * q + h
            for a in range(16):
                wa[b, a] = mixed(yb[b, a], zp[b, a], sb[2, b, a])
            source, target = wa, wb
            for level, bit in enumerate((8, 4, 2, 1)):
                for a in range(16):
                    if a & bit == 0:
                        out_a, out_b = mixed_pair(
                            source[b, a], source[b, a | bit], tb[level, a, b], tb[level, a | bit, b]
                        )
                        target[b, a] = out_a
                        target[b, a | bit] = out_b
                source, target = target, source
            out[xz, b] = wa[b, xz]
        for k in range(15):
            r_copy(q, k).start()
        return carry

    lax.fori_loop(0, 4, last_body, 0)

    for q in range(4):
        for k in range(15):
            r_copy(q, k).wait()
        p_copy(q).wait_send()
        z_copy(q).wait_send()
        for r in yc_offsets:
            y_copy(q, r).wait_send()
    for level in range(3):
        for r in yc_offsets:
            s_copy(level, r).wait_send()
    for k in range(15):
        t_copy(k).wait_send()


def local(source_values, leaf_maps, source_transfers, target_transfers):
    dma = pltpu.SemaphoreType.DMA
    boxes = (32, 128)
    out = pl.pallas_call(
        kernel,
        out_shape=jax.ShapeDtypeStruct((16, 8) + boxes, BF16),
        in_specs=[pl.BlockSpec(memory_space=pl.ANY)] * 4,
        out_specs=pl.BlockSpec(memory_space=pltpu.VMEM),
        scratch_shapes=[
            pltpu.VMEM((16, 8, 64, 128), BF16),
            pltpu.VMEM((16, 8) + boxes, BF16),
            pltpu.VMEM((16, 8) + boxes, BF16),
            pltpu.VMEM((3, 8, 16) + boxes, BF16),
            pltpu.VMEM((4, 16, 8) + boxes, BF16),
            pltpu.VMEM((16, 8) + boxes, BF16),
            pltpu.VMEM((16, 8) + boxes, BF16),
            pltpu.VMEM((8, 16) + boxes, BF16),
            pltpu.VMEM((8, 16) + boxes, BF16),
            pltpu.VMEM((8, 16) + boxes, BF16),
            pltpu.VMEM((8, 16) + boxes, BF16),
            pltpu.VMEM((8, 16) + boxes, BF16),
            pltpu.VMEM((8, 16) + boxes, BF16),
            pltpu.VMEM((8, 16) + boxes, BF16),
            dma((3,)),
            dma((4,)),
            dma((3, 8)),
            dma((3, 8)),
            dma((15,)),
            dma((15,)),
            dma((4,)),
            dma((4,)),
            dma((4, 8)),
            dma((4, 8)),
            dma((4,)),
            dma((4,)),
            dma((4, 15)),
            dma((4, 15)),
        ],
        compiler_params=pltpu.CompilerParams(
            collective_id=0, has_side_effects=True, vmem_limit_bytes=67_043_328
        ),
    )(
        source_values.reshape(16, 8, 64, 128),
        leaf_maps.reshape((16, 8) + boxes),
        source_transfers.reshape((4, 16, 8) + boxes),
        target_transfers.reshape((4, 16, 8) + boxes),
    )
    return out.reshape((128,) + boxes)


def solution(mesh):
    return jax.shard_map(
        local,
        mesh=mesh,
        in_specs=(
            P(("gx", "gy"), None, None),
            P(("gx", "gy"), None, None),
            P(None, ("gx", "gy"), None, None),
            P(None, ("gx", "gy"), None, None),
        ),
        out_specs=P(("gx", "gy"), None, None),
        check_vma=False,
    )
```

time: 270 us -> 116 us (0.43)
  the two profiles are of different devices: /device:TPU:4 before, /device:TPU:1 now
where the time goes in v1:
time: 116 us
  Pallas kernels  114 us (98%)
  local copies, waits for them, and re-layouts  2.26 us (2%)
    pallas_call x1, Pallas kernels, local(): pl.pallas_call(kernel, out_shape=jax.ShapeDtypeStruct((16, 8) + boxes, BF...  114 us

profile of v1, /device:TPU:1, one launch (start us, length us, event | category | flops | bytes accessed | tf_op | source)
XLA Modules:
  0.0 116.1 jit_solution(12860124152837286610)
XLA Ops:
  0.0 113.9 %shard_map.46 = bf16[16,8,32,128]{3,2,1,0:T(8,128)(2,1)} custom-call(bf16[16,8,64,128]{3,2,1,0:T(8,128)(2,1)} %bitcast.8, bf16[16,8,32,128]{3,2,1,0:T(8,128)(2,1)} %bitcast.9, bf16[4,16,8,32,128]{4,3,2,1,0:T(8,128)(2,1)} %bitcast.5, bf16[4,16,8,32,128]{4,3,2,1,0:T(8,128)(2,1)} %bitcast.6), custom_call_target="tpu_custom_call" | custom-call | tf_op jit(solution)/shard_map/pallas_call | solution.py:261
  113.9 2.3 %copy.6 = bf16[128,32,128]{2,1,0:T(8,128)(2,1)} copy(bf16[128,32,128]{2,1,0:T(8,128)(2,1)} %bitcast.7) | data formatting | bytes 2097152

commit v2 on v0

v2 whole, which is shorter than its diff:
```python
import jax
import jax.numpy as jnp
from jax import lax
from jax.experimental import pallas as pl
from jax.experimental.pallas import tpu as pltpu
from jax.sharding import PartitionSpec as P

MESH = pl.DeviceIdType.MESH
BF16 = jnp.bfloat16
F32 = jnp.float32


def turned(x):
    wide = pltpu.roll(x.astype(F32), 64, x.ndim - 1)
    lane = lax.broadcasted_iota(jnp.int32, wide.shape, wide.ndim - 1)
    return jnp.where(lane < 64, -wide, wide).astype(BF16)


def dot(a, b):
    return jnp.dot(a, b, preferred_element_type=F32).astype(BF16)


def mixed(own, partner, transfer):
    operand = jnp.concatenate([own, turned(own), partner, turned(partner)], axis=0)
    return dot(transfer, operand)


def mixed_pair(a, b, transfer_a, transfer_b):
    ta, tb = turned(a), turned(b)
    out_a = dot(transfer_a, jnp.concatenate([a, ta, b, tb], axis=0))
    out_b = dot(transfer_b, jnp.concatenate([b, tb, a, ta], axis=0))
    return out_a, out_b


def paired(values, bit, transfer):
    result = [None] * len(values)
    for n in range(len(values)):
        if n & bit == 0:
            m = n | bit
            result[n], result[m] = mixed_pair(values[n], values[m], transfer(n), transfer(m))
    return result


def kernel(
    src, leaf, st, tt, out,
    src_v, leaf_v, s0, sb, sk, sp, t01, t23, c0, c0p, c1, cb, yk, ys, yp, wm, mb, rb,
    load_sem, own_sem, s_send, s_recv, s3_send, s3_recv, t01_send, t01_recv, t23_send, t23_recv,
    p_send, p_recv, y_send, y_recv, z_send, z_recv, m_send, m_recv, r_send, r_recv,
):
    x = lax.axis_index("gx")
    g = lax.axis_index("gy")
    z = g // 8
    z1 = z // 2
    z0 = z % 2
    a = (z0 + z1) % 2
    other = 1 - a
    yc = g % 8
    core = g % 2
    mate = z + 1 - 2 * z0

    def z_of(a_bit, k):
        return 2 * k + (a_bit + k) % 2

    def remote(source, target, send, recv, device):
        return pltpu.make_async_remote_copy(
            src_ref=source,
            dst_ref=target,
            send_sem=send,
            recv_sem=recv,
            device_id=device,
            device_id_type=MESH,
        )

    def s_copy(level, r):
        to = (yc + r) % 8
        return remote(
            st.at[level + 1, :, :, to],
            sb.at[level, yc],
            s_send.at[level, r],
            s_recv.at[level, r],
            (x, z * 8 + to),
        )

    def s3_copy(far, k, r):
        to = (yc + r) % 8
        return remote(
            st.at[3, :, z_of(other if far else a, k), to],
            (sp if far else sk).at[yc, k],
            s3_send.at[far, k, r],
            s3_recv.at[far, k, r],
            (x, (mate if far else z) * 8 + to),
        )

    def t01_copy(level, i, h):
        to_x = (x + i) % 4
        to_z1 = (z1 + h) % 2
        return remote(
            tt.at[level, to_x, to_z1],
            t01.at[level, x, z1],
            t01_send.at[level, i, h],
            t01_recv.at[level, i, h],
            (to_x, z_of(a, to_z1) * 8 + yc),
        )

    def t23_copy(level, j):
        to_z = (z + j) % 4
        return remote(
            tt.at[level + 2, :, to_z // 2, to_z % 2],
            t23.at[level, z],
            t23_send.at[level, j],
            t23_recv.at[level, j],
            (x, to_z * 8 + yc),
        )

    def p_copy(q):
        return remote(
            c0.at[q], c0p.at[q], p_send.at[q], p_recv.at[q], (x, g + 1 - 2 * core)
        )

    def y_copy(q, r):
        to = (yc + r) % 8
        return remote(
            c1.at[to, q], cb.at[yc, q], y_send.at[q, r], y_recv.at[q, r], (x, z * 8 + to)
        )

    def z_copy(q):
        chunk = pl.ds(2 * q, 2)
        return remote(
            ys.at[chunk], yp.at[chunk], z_send.at[q], z_recv.at[q], (x, mate * 8 + yc)
        )

    def m_copy(q, i, h):
        chunk = pl.ds(2 * q, 2)
        to_x = (x + i) % 4
        to_z0 = (z0 + h) % 2
        return remote(
            wm.at[to_z0, to_x, chunk],
            mb.at[x, a, chunk],
            m_send.at[q, i, h],
            m_recv.at[q, i, h],
            (to_x, (2 * z1 + to_z0) * 8 + yc),
        )

    def r_copy(q, j):
        chunk = pl.ds(2 * q, 2)
        to_z = (z + j) % 4
        return remote(
            rb.at[to_z, :, chunk],
            out.at[:, z, chunk],
            r_send.at[q, j],
            r_recv.at[q, j],
            (x, to_z * 8 + yc),
        )

    near = [(i, h) for h in range(2) for i in (1, 3, 2, 0) if (i, h) != (0, 0)]
    along_y = [2, 6, 4, 1, 3, 7, 5]
    along_z = [1, 3, 2]
    s3_all = [(far, k, r) for r in [0] + along_y for far in (0, 1) for k in (0, 1)]
    s3_sent = [(far, k, r) for far, k, r in s3_all if (far, r) != (0, 0)]

    loads = [
        pltpu.make_async_copy(src, src_v, load_sem.at[0]),
        pltpu.make_async_copy(leaf, leaf_v, load_sem.at[1]),
        pltpu.make_async_copy(st.at[0], s0, load_sem.at[2]),
    ]
    for copy in loads:
        copy.start()
    own_s = [
        pltpu.make_async_copy(st.at[n + 1, :, :, yc], sb.at[n, yc], own_sem.at[n])
        for n in range(2)
    ]
    own_s3 = [
        pltpu.make_async_copy(st.at[3, :, z_of(a, k), yc], sk.at[yc, k], own_sem.at[2 + k])
        for k in range(2)
    ]
    own_t = [
        pltpu.make_async_copy(tt.at[n, x, z1], t01.at[n, x, z1], own_sem.at[4 + n])
        for n in range(2)
    ] + [
        pltpu.make_async_copy(tt.at[n + 2, :, z1, z0], t23.at[n, z], own_sem.at[6 + n])
        for n in range(2)
    ]
    for copy in own_s + own_s3 + own_t:
        copy.start()

    barrier = pltpu.get_barrier_semaphore()
    peers = [(x, z * 8 + (yc + r) % 8) for r in range(1, 8)]
    peers += [(x, mate * 8 + (yc + r) % 8) for r in range(8)]
    peers += [(x, ((z + 2) % 4) * 8 + yc), (x, ((mate + 2) % 4) * 8 + yc)]
    for i in range(1, 4):
        for to_z in (z, mate, z_of(a, 1 - z1)):
            peers.append(((x + i) % 4, to_z * 8 + yc))
    for peer in peers:
        pl.semaphore_signal(barrier, inc=1, device_id=peer, device_id_type=MESH)

    loads[0].wait()
    loads[1].wait()

    def leaf_body(n, carry):
        for i in range(8):
            v = src_v[n // 4, n % 4, i]
            c0[n // 4, n % 4, i] = dot(
                leaf_v[n // 4, n % 4, i], jnp.concatenate([v, turned(v)], axis=0)
            )
        return carry

    lax.fori_loop(0, 16, leaf_body, 0)
    pl.semaphore_wait(barrier, len(peers))

    for q in range(4):
        p_copy(q).start()
    for level in range(2):
        for r in along_y:
            s_copy(level, r).start()
    for level in range(2):
        for i, h in near:
            t01_copy(level, i, h).start()
        for j in along_z:
            t23_copy(level, j).start()

    loads[2].wait()

    def first_body(q, carry):
        p_copy(q).wait_recv()
        for n in range(4):
            for i in range(8):
                c1[i, q, n] = mixed(c0[q, n, i], c0p[q, n, i], s0[q, n, i])
        for r in along_y:
            y_copy(q, r).start()
        return carry

    lax.fori_loop(0, 4, first_body, 0)
    for far, k, r in s3_sent:
        s3_copy(far, k, r).start()
    cb[yc] = c1[yc]

    for level in range(2):
        own_s[level].wait()
        for r in along_y:
            s_copy(level, r).wait_recv()

    def y_body(q, carry):
        for r in along_y:
            y_copy(q, r).wait_recv()
        for k in range(2):
            for target, a_bit in ((ys, other), (yk, a)):
                vz = z_of(a_bit, k)
                values = [cb[i, q, vz] for i in range(8)]
                for level, bit in enumerate((2, 4)):
                    values = paired(values, bit, lambda i: sb[level, i, q, vz])
                for i in range(8):
                    target[i, k, q] = values[i]
        return carry

    lax.fori_loop(0, 4, y_body, 0)
    for q in range(4):
        z_copy(q).start()
    for copy in own_s3 + own_t:
        copy.wait()
    for far, k, r in s3_sent:
        s3_copy(far, k, r).wait_recv()
    for level in range(2):
        for i, h in near:
            t01_copy(level, i, h).wait_recv()

    def x_body(q, carry):
        z_copy(q).wait_recv()
        for b in range(2):
            i = 2 * q + b
            for k in range(2):
                values = [yk[i, k, n] for n in range(4)] + [yp[i, k, n] for n in range(4)]
                values = paired(
                    values, 4, lambda n: sp[i, k, n - 4] if n >= 4 else sk[i, k, n]
                )
                sides = (z0, 1 - z0)
                for level, bit in enumerate((2, 1)):
                    values = paired(
                        values, bit, lambda n: t01[level, n % 4, k, sides[n // 4], i]
                    )
                for n in range(8):
                    wm[sides[n // 4], n % 4, i, k] = values[n]
        for i, h in near:
            m_copy(q, i, h).start()
        chunk = pl.ds(2 * q, 2)
        mb[x, a, chunk] = wm[z0, x, chunk]
        return carry

    lax.fori_loop(0, 4, x_body, 0)
    for level in range(2):
        for j in along_z:
            t23_copy(level, j).wait_recv()

    def last_body(q, carry):
        for i, h in near:
            m_copy(q, i, h).wait_recv()
        for b in range(2):
            i = 2 * q + b
            for n in range(4):
                values = [mb[n, m // 2, i, m % 2] for m in range(4)]
                for level, bit in enumerate((3, 2)):
                    result = [None] * 4
                    for m in range(2):
                        w = m ^ bit
                        result[m], result[w] = mixed_pair(
                            values[m],
                            values[w],
                            t23[level, z_of(m // 2, m % 2), n, i],
                            t23[level, z_of(w // 2, w % 2), n, i],
                        )
                    values = result
                for m in range(4):
                    rb[z_of(m // 2, m % 2), n, i] = values[m]
        for j in along_z:
            r_copy(q, j).start()
        chunk = pl.ds(2 * q, 2)
        out[:, z, chunk] = rb[z, :, chunk]
        return carry

    lax.fori_loop(0, 4, last_body, 0)

    for q in range(4):
        for j in along_z:
            r_copy(q, j).wait()
        for i, h in near:
            m_copy(q, i, h).wait_send()
        p_copy(q).wait_send()
        z_copy(q).wait_send()
        for r in along_y:
            y_copy(q, r).wait_send()
    for level in range(2):
        for r in along_y:
            s_copy(level, r).wait_send()
        for i, h in near:
            t01_copy(level, i, h).wait_send()
        for j in along_z:
            t23_copy(level, j).wait_send()
    for far, k, r in s3_sent:
        s3_copy(far, k, r).wait_send()


def local(source_values, leaf_maps, source_transfers, target_transfers):
    dma = pltpu.SemaphoreType.DMA
    box = (32, 128)

    def vmem(*shape):
        return pltpu.VMEM(shape + box, BF16)

    out = pl.pallas_call(
        kernel,
        out_shape=jax.ShapeDtypeStruct((4, 4, 8) + box, BF16),
        in_specs=[pl.BlockSpec(memory_space=pl.ANY)] * 4,
        out_specs=pl.BlockSpec(memory_space=pltpu.VMEM),
        scratch_shapes=[
            pltpu.VMEM((4, 4, 8, 64, 128), BF16),
            vmem(4, 4, 8),
            vmem(4, 4, 8),
            vmem(2, 8, 4, 4),
            vmem(8, 2, 4),
            vmem(8, 2, 4),
            vmem(2, 4, 2, 2, 8),
            vmem(2, 4, 4, 8),
            vmem(4, 4, 8),
            vmem(4, 4, 8),
            vmem(8, 4, 4),
            vmem(8, 4, 4),
            vmem(8, 2, 4),
            vmem(8, 2, 4),
            vmem(8, 2, 4),
            vmem(2, 4, 8, 2),
            vmem(4, 2, 8, 2),
            vmem(4, 4, 8),
            dma((3,)),
            dma((8,)),
            dma((2, 8)),
            dma((2, 8)),
            dma((2, 2, 8)),
            dma((2, 2, 8)),
            dma((2, 4, 2)),
            dma((2, 4, 2)),
            dma((2, 4)),
            dma((2, 4)),
            dma((4,)),
            dma((4,)),
            dma((4, 8)),
            dma((4, 8)),
            dma((4,)),
            dma((4,)),
            dma((4, 4, 2)),
            dma((4, 4, 2)),
            dma((4, 4)),
            dma((4, 4)),
        ],
        compiler_params=pltpu.CompilerParams(
            collective_id=0, has_side_effects=True, vmem_limit_bytes=67_043_328
        ),
    )(
        source_values.reshape(4, 4, 8, 64, 128),
        leaf_maps.reshape((4, 4, 8) + box),
        source_transfers.reshape((4, 4, 4, 8) + box),
        target_transfers.reshape((4, 4, 2, 2, 8) + box),
    )
    return out.reshape((128,) + box)


def solution(mesh):
    return jax.shard_map(
        local,
        mesh=mesh,
        in_specs=(
            P(("gx", "gy"), None, None),
            P(("gx", "gy"), None, None),
            P(None, ("gx", "gy"), None, None),
            P(None, ("gx", "gy"), None, None),
        ),
        out_specs=P(("gx", "gy"), None, None),
        check_vma=False,
    )
```

time: 270 us -> 101 us (0.37)
  waiting for transfers between devices: 142 us -> 0 us
  Pallas kernels: 0 us -> 97.4 us
  local copies, waits for them, and re-layouts: 52.9 us -> 2.26 us
  matrix products: 30 us -> 0 us
  blocking collectives: 27.6 us -> 0 us
  starting transfers between devices: 12.8 us -> 0 us
  other arithmetic: 3.65 us -> 0 us
    ppermute x8 -> x0, waiting for transfers between devices: 142 us -> none  [swapped(): return lax.ppermute(block, axis, route)]
    pallas_call x0 -> x1, Pallas kernels: none -> 97.4 us  [local(): pl.pallas_call(kernel, out_shape=jax.ShapeDtypeStruct((4, 4, 8) + box, BF...]
    reshape x17 -> x0, local copies, waits for them, and re-layouts: 30 us -> none  [rotated(): return turned.reshape(block.shape)]
    dot_general x9 -> x0, matrix products: 30 us -> none  [complex_apply(): jnp.einsum('bik,bkc->bic', matrix, operand, preferred_element_type=jnp.fl...]
    all_to_all x1 -> x0, blocking collectives: 27.6 us -> none  [local(): lax.all_to_all(coeffs, ('gx', 'gy'), split_axis=0, concat_axis=0, tiled=T...]
    ppermute x8 -> x0, starting transfers between devices: 12.8 us -> none  [swapped(): return lax.ppermute(block, axis, route)]
    ppermute x8 -> x0, local copies, waits for them, and re-layouts: 11.7 us -> none  [swapped(): return lax.ppermute(block, axis, route)]
    convert_element_type x7 -> x0, local copies, waits for them, and re-layouts: 6.81 us -> none  [complex_apply(): jnp.einsum('bik,bkc->bic', matrix, operand, preferred_element_type=jnp.fl...]
  transfers between devices with their start and end apart: 8 -> 0, of which waited for: 7 -> 0; matrix products, arithmetic and copies ran while one was open for 9% -> 0% of each run, Pallas kernels for 0% -> 0%
where the time goes in v2:
time: 101 us; the launch traced here: 99.7 us
  Pallas kernels  97.4 us (96%)
  local copies, waits for them, and re-layouts  2.26 us (2%)
    pallas_call x1, Pallas kernels, local(): pl.pallas_call(kernel, out_shape=jax.ShapeDtypeStruct((4, 4, 8) + box, BF...  97.4 us
    unnamed x1, local copies, waits for them, and re-layouts  2.26 us

profile of v2, /device:TPU:4, one launch (start us, length us, event | category | flops | bytes accessed | tf_op | source)
XLA Modules:
  0.0 99.7 jit_solution(10335586071561829256)
XLA Ops:
  0.0 97.4 %shard_map.46 = bf16[4,4,8,32,128]{4,3,2,1,0:T(8,128)(2,1)} custom-call(bf16[4,4,8,64,128]{4,3,2,1,0:T(8,128)(2,1)} %bitcast.8, bf16[4,4,8,32,128]{4,3,2,1,0:T(8,128)(2,1)} %bitcast.9, bf16[4,4,4,8,32,128]{5,4,3,2,1,0:T(8,128)(2,1)} %bitcast.5, bf16[4,4,2,2,8,32,128]{6,5,4,3,2,1,0:T(8,128)(2,1)} %bitcast.6), custom_call_target="tpu_custom_call" | custom-call | tf_op jit(solution)/shard_map/pallas_call | solution.py:348
  97.4 2.3 %copy.6 = bf16[128,32,128]{2,1,0:T(8,128)(2,1)} copy(bf16[128,32,128]{2,1,0:T(8,128)(2,1)} %bitcast.7) | data formatting | bytes 2097152

commit v3 on v2

v3 whole, which is shorter than its diff:
```python
import jax
import jax.numpy as jnp
from jax import lax
from jax.experimental import pallas as pl
from jax.experimental.pallas import tpu as pltpu
from jax.sharding import PartitionSpec as P

MESH = pl.DeviceIdType.MESH
BF16 = jnp.bfloat16
F32 = jnp.float32


def turned(x):
    wide = pltpu.roll(x.astype(F32), 64, x.ndim - 1)
    lane = lax.broadcasted_iota(jnp.int32, wide.shape, wide.ndim - 1)
    return jnp.where(lane < 64, -wide, wide).astype(BF16)


def dot(a, b):
    return jnp.dot(a, b, preferred_element_type=F32).astype(BF16)


def mixed(own, partner, transfer):
    operand = jnp.concatenate([own, turned(own), partner, turned(partner)], axis=0)
    return dot(transfer, operand)


def mixed_pair(a, b, transfer_a, transfer_b):
    ta, tb = turned(a), turned(b)
    out_a = dot(transfer_a, jnp.concatenate([a, ta, b, tb], axis=0))
    out_b = dot(transfer_b, jnp.concatenate([b, tb, a, ta], axis=0))
    return out_a, out_b


def paired(values, bit, transfer):
    result = [None] * len(values)
    for n in range(len(values)):
        if n & bit == 0:
            m = n | bit
            result[n], result[m] = mixed_pair(values[n], values[m], transfer(n), transfer(m))
    return result


NH = 4
CH = 8 // NH


def kernel(
    src, leaf, st, tt, out,
    src_v, leaf_v, s0, sb, sk, sp, t01, t23, c0, c0p, c1, cb, yk, ys, yp, wm, mb, rb,
    load_sem, own_sem, s_send, s_recv, s3_send, s3_recv, t01_send, t01_recv, t23_send, t23_recv,
    p_send, p_recv, y_send, y_recv, z_send, z_recv, m_send, m_recv, r_send, r_recv,
):
    x = lax.axis_index("gx")
    g = lax.axis_index("gy")
    z = g // 8
    z1 = z // 2
    z0 = z % 2
    a = (z0 + z1) % 2
    other = 1 - a
    yc = g % 8
    core = g % 2
    mate = z + 1 - 2 * z0

    def z_of(a_bit, k):
        return 2 * k + (a_bit + k) % 2

    def remote(source, target, send, recv, device):
        return pltpu.make_async_remote_copy(
            src_ref=source,
            dst_ref=target,
            send_sem=send,
            recv_sem=recv,
            device_id=device,
            device_id_type=MESH,
        )

    def s_copy(level, k, r):
        to = (yc + r) % 8
        return remote(
            st.at[level + 1, :, k, :, to],
            sb.at[level, yc, k],
            s_send.at[level, k, r],
            s_recv.at[level, k, r],
            (x, z * 8 + to),
        )

    def s3_copy(far, k, r):
        to = (yc + r) % 8
        return remote(
            st.at[3, :, k, ((other if far else a) + k) % 2, to],
            (sp if far else sk).at[yc, k],
            s3_send.at[far, k, r],
            s3_recv.at[far, k, r],
            (x, (mate if far else z) * 8 + to),
        )

    def t01_copy(level, i, h):
        to_x = (x + i) % 4
        to_z1 = (z1 + h) % 2
        return remote(
            tt.at[level, to_x, to_z1],
            t01.at[level, x, z1],
            t01_send.at[level, i, h],
            t01_recv.at[level, i, h],
            (to_x, z_of(a, to_z1) * 8 + yc),
        )

    def t23_copy(level, j):
        to_z = (z + j) % 4
        return remote(
            tt.at[level + 2, :, to_z // 2, to_z % 2],
            t23.at[level, z],
            t23_send.at[level, j],
            t23_recv.at[level, j],
            (x, to_z * 8 + yc),
        )

    def p_copy(k):
        return remote(
            c0.at[k], c0p.at[k], p_send.at[k], p_recv.at[k], (x, g + 1 - 2 * core)
        )

    def y_copy(k, r):
        to = (yc + r) % 8
        return remote(
            c1.at[to, k], cb.at[yc, k], y_send.at[k, r], y_recv.at[k, r], (x, z * 8 + to)
        )

    def z_copy(k, q):
        chunk = pl.ds(CH * q, CH)
        return remote(
            ys.at[k, chunk], yp.at[k, chunk], z_send.at[k, q], z_recv.at[k, q], (x, mate * 8 + yc)
        )

    def m_copy(k, q, i, h):
        chunk = pl.ds(CH * q, CH)
        to_x = (x + i) % 4
        to_z0 = (z0 + h) % 2
        return remote(
            wm.at[to_z0, to_x, k, chunk],
            mb.at[x, a, k, chunk],
            m_send.at[k, q, i, h],
            m_recv.at[k, q, i, h],
            (to_x, (2 * z1 + to_z0) * 8 + yc),
        )

    def r_copy(q, j):
        chunk = pl.ds(CH * q, CH)
        to_z = (z + j) % 4
        return remote(
            rb.at[to_z, :, chunk],
            out.at[:, z, chunk],
            r_send.at[q, j],
            r_recv.at[q, j],
            (x, to_z * 8 + yc),
        )

    near = [(i, h) for h in range(2) for i in (1, 3, 2, 0) if (i, h) != (0, 0)]
    along_y = [2, 6, 4, 1, 3, 7, 5]
    along_z = [1, 3, 2]
    s3_sent = [(far, r) for r in [0] + along_y for far in (0, 1) if (far, r) != (0, 0)]

    loads = [
        pltpu.make_async_copy(src, src_v, load_sem.at[0]),
        pltpu.make_async_copy(leaf, leaf_v, load_sem.at[1]),
        pltpu.make_async_copy(st.at[0], s0, load_sem.at[2]),
    ]
    for copy in loads:
        copy.start()
    own_s = [
        pltpu.make_async_copy(st.at[n + 1, :, k, :, yc], sb.at[n, yc, k], own_sem.at[2 * k + n])
        for k in range(2)
        for n in range(2)
    ]
    own_s3 = [
        pltpu.make_async_copy(st.at[3, :, k, (a + k) % 2, yc], sk.at[yc, k], own_sem.at[4 + k])
        for k in range(2)
    ]
    own_t = [
        pltpu.make_async_copy(tt.at[n, x, z1], t01.at[n, x, z1], own_sem.at[6 + n])
        for n in range(2)
    ] + [
        pltpu.make_async_copy(tt.at[n + 2, :, z1, z0], t23.at[n, z], own_sem.at[8 + n])
        for n in range(2)
    ]
    for copy in own_s + own_s3 + own_t:
        copy.start()

    barrier = pltpu.get_barrier_semaphore()
    peers = [(x, z * 8 + (yc + r) % 8) for r in range(1, 8)]
    peers += [(x, mate * 8 + (yc + r) % 8) for r in range(8)]
    peers += [(x, ((z + 2) % 4) * 8 + yc), (x, ((mate + 2) % 4) * 8 + yc)]
    for i in range(1, 4):
        for to_z in (z, mate, z_of(a, 1 - z1)):
            peers.append(((x + i) % 4, to_z * 8 + yc))
    for peer in peers:
        pl.semaphore_signal(barrier, inc=1, device_id=peer, device_id_type=MESH)

    loads[0].wait()
    loads[1].wait()

    def leaf_body(n, carry):
        vx, k, j = n // 4, n // 2 % 2, n % 2
        for i in range(8):
            v = src_v[vx, k, j, i]
            c0[k, vx, j, i] = dot(leaf_v[vx, k, j, i], jnp.concatenate([v, turned(v)], axis=0))
        return carry

    lax.fori_loop(0, 16, leaf_body, 0)
    pl.semaphore_wait(barrier, len(peers))

    for k in range(2):
        p_copy(k).start()
    for level in range(2):
        for r in along_y:
            s_copy(level, 0, r).start()
    for level in range(2):
        for i, h in near:
            t01_copy(level, i, h).start()
    for level in range(2):
        for j in along_z:
            t23_copy(level, j).start()

    loads[2].wait()
    for k in range(2):
        p_copy(k).wait_recv()

        def first_body(vx, carry, k=k):
            for j in range(2):
                for i in range(8):
                    c1[i, k, vx, j] = mixed(c0[k, vx, j, i], c0p[k, vx, j, i], s0[vx, k, j, i])
            return carry

        lax.fori_loop(0, 4, first_body, 0)
        if k == 1:
            for level in range(2):
                for r in along_y:
                    s_copy(level, 1, r).start()
        for r in along_y:
            y_copy(k, r).start()
        for far, r in s3_sent:
            s3_copy(far, k, r).start()
        cb[yc, k] = c1[yc, k]

    for k in range(2):
        for level in range(2):
            own_s[2 * k + level].wait()
            for r in along_y:
                s_copy(level, k, r).wait_recv()
        for r in along_y:
            y_copy(k, r).wait_recv()

        def y_body(vx, carry, k=k):
            for target, a_bit in ((ys, other), (yk, a)):
                j = (a_bit + k) % 2
                values = [cb[i, k, vx, j] for i in range(8)]
                for level, bit in enumerate((2, 4)):
                    values = paired(values, bit, lambda i: sb[level, i, k, vx, j])
                for i in range(8):
                    target[k, i, vx] = values[i]
            return carry

        lax.fori_loop(0, 4, y_body, 0)
        for q in range(NH):
            z_copy(k, q).start()

        own_s3[k].wait()
        for far, r in s3_sent:
            s3_copy(far, k, r).wait_recv()
        if k == 0:
            for copy in own_t:
                copy.wait()
            for level in range(2):
                for i, h in near:
                    t01_copy(level, i, h).wait_recv()

        sides = (z0, 1 - z0)

        def x_body(q, carry, k=k):
            z_copy(k, q).wait_recv()
            for b in range(CH):
                i = CH * q + b
                values = [yk[k, i, n] for n in range(4)] + [yp[k, i, n] for n in range(4)]
                values = paired(
                    values, 4, lambda n: sp[i, k, n - 4] if n >= 4 else sk[i, k, n]
                )
                for level, bit in enumerate((2, 1)):
                    values = paired(
                        values, bit, lambda n: t01[level, n % 4, k, sides[n // 4], i]
                    )
                for n in range(8):
                    wm[sides[n // 4], n % 4, k, i] = values[n]
            for i, h in near:
                m_copy(k, q, i, h).start()
            chunk = pl.ds(CH * q, CH)
            mb[x, a, k, chunk] = wm[z0, x, k, chunk]
            return carry

        lax.fori_loop(0, NH, x_body, 0)

    for level in range(2):
        for j in along_z:
            t23_copy(level, j).wait_recv()

    def last_body(q, carry):
        for k in range(2):
            for i, h in near:
                m_copy(k, q, i, h).wait_recv()
        for b in range(CH):
            i = CH * q + b
            for n in range(4):
                values = [mb[n, m // 2, m % 2, i] for m in range(4)]
                for level, bit in enumerate((3, 2)):
                    result = [None] * 4
                    for m in range(2):
                        w = m ^ bit
                        result[m], result[w] = mixed_pair(
                            values[m],
                            values[w],
                            t23[level, z_of(m // 2, m % 2), n, i],
                            t23[level, z_of(w // 2, w % 2), n, i],
                        )
                    values = result
                for m in range(4):
                    rb[z_of(m // 2, m % 2), n, i] = values[m]
        for j in along_z:
            r_copy(q, j).start()
        chunk = pl.ds(CH * q, CH)
        out[:, z, chunk] = rb[z, :, chunk]
        return carry

    lax.fori_loop(0, NH, last_body, 0)

    for q in range(NH):
        for j in along_z:
            r_copy(q, j).wait()
        for k in range(2):
            z_copy(k, q).wait_send()
            for i, h in near:
                m_copy(k, q, i, h).wait_send()
    for k in range(2):
        p_copy(k).wait_send()
        for r in along_y:
            y_copy(k, r).wait_send()
            for level in range(2):
                s_copy(level, k, r).wait_send()
        for far, r in s3_sent:
            s3_copy(far, k, r).wait_send()
    for level in range(2):
        for i, h in near:
            t01_copy(level, i, h).wait_send()
        for j in along_z:
            t23_copy(level, j).wait_send()


def local(source_values, leaf_maps, source_transfers, target_transfers):
    dma = pltpu.SemaphoreType.DMA
    box = (32, 128)

    def vmem(*shape):
        return pltpu.VMEM(shape + box, BF16)

    out = pl.pallas_call(
        kernel,
        out_shape=jax.ShapeDtypeStruct((4, 4, 8) + box, BF16),
        in_specs=[pl.BlockSpec(memory_space=pl.ANY)] * 4,
        out_specs=pl.BlockSpec(memory_space=pltpu.VMEM),
        scratch_shapes=[
            pltpu.VMEM((4, 2, 2, 8, 64, 128), BF16),
            vmem(4, 2, 2, 8),
            vmem(4, 2, 2, 8),
            vmem(2, 8, 2, 4, 2),
            vmem(8, 2, 4),
            vmem(8, 2, 4),
            vmem(2, 4, 2, 2, 8),
            vmem(2, 4, 4, 8),
            vmem(2, 4, 2, 8),
            vmem(2, 4, 2, 8),
            vmem(8, 2, 4, 2),
            vmem(8, 2, 4, 2),
            vmem(2, 8, 4),
            vmem(2, 8, 4),
            vmem(2, 8, 4),
            vmem(2, 4, 2, 8),
            vmem(4, 2, 2, 8),
            vmem(4, 4, 8),
            dma((3,)),
            dma((10,)),
            dma((2, 2, 8)),
            dma((2, 2, 8)),
            dma((2, 2, 8)),
            dma((2, 2, 8)),
            dma((2, 4, 2)),
            dma((2, 4, 2)),
            dma((2, 4)),
            dma((2, 4)),
            dma((2,)),
            dma((2,)),
            dma((2, 8)),
            dma((2, 8)),
            dma((2, NH)),
            dma((2, NH)),
            dma((2, NH, 4, 2)),
            dma((2, NH, 4, 2)),
            dma((NH, 4)),
            dma((NH, 4)),
        ],
        compiler_params=pltpu.CompilerParams(
            collective_id=0, has_side_effects=True, vmem_limit_bytes=67_043_328
        ),
    )(
        source_values.reshape(4, 2, 2, 8, 64, 128),
        leaf_maps.reshape((4, 2, 2, 8) + box),
        source_transfers.reshape((4, 4, 2, 2, 8) + box),
        target_transfers.reshape((4, 4, 2, 2, 8) + box),
    )
    return out.reshape((128,) + box)


def solution(mesh):
    return jax.shard_map(
        local,
        mesh=mesh,
        in_specs=(
            P(("gx", "gy"), None, None),
            P(("gx", "gy"), None, None),
            P(None, ("gx", "gy"), None, None),
            P(None, ("gx", "gy"), None, None),
        ),
        out_specs=P(("gx", "gy"), None, None),
        check_vma=False,
    )
```

time: 101 us -> 99.2 us (0.982)
  Pallas kernels: 97.4 us -> 95.6 us
    pallas_call x1, Pallas kernels: 97.4 us -> 95.6 us  [local(): pl.pallas_call(kernel, out_shape=jax.ShapeDtypeStruct((4, 4, 8) + box, BF...]
where the time goes in v3:
time: 99.2 us; the launch traced here: 97.9 us
  Pallas kernels  95.6 us (96%)
  local copies, waits for them, and re-layouts  2.26 us (2%)
    pallas_call x1, Pallas kernels, local(): pl.pallas_call(kernel, out_shape=jax.ShapeDtypeStruct((4, 4, 8) + box, BF...  95.6 us
    unnamed x1, local copies, waits for them, and re-layouts  2.26 us

profile of v3, /device:TPU:4, one launch (start us, length us, event | category | flops | bytes accessed | tf_op | source)
XLA Modules:
  0.0 97.9 jit_solution(17450508285157708499)
XLA Ops:
  0.0 95.6 %shard_map.46 = bf16[4,4,8,32,128]{4,3,2,1,0:T(8,128)(2,1)} custom-call(bf16[4,2,2,8,64,128]{5,4,3,2,1,0:T(8,128)(2,1)} %bitcast.8, bf16[4,2,2,8,32,128]{5,4,3,2,1,0:T(8,128)(2,1)} %bitcast.9, bf16[4,4,2,2,8,32,128]{6,5,4,3,2,1,0:T(8,128)(2,1)} %bitcast.5, bf16[4,4,2,2,8,32,128]{6,5,4,3,2,1,0:T(8,128)(2,1)} %bitcast.6), custom_call_target="tpu_custom_call" | custom-call | tf_op jit(solution)/shard_map/pallas_call | solution.py:364
  95.6 2.3 %copy.6 = bf16[128,32,128]{2,1,0:T(8,128)(2,1)} copy(bf16[128,32,128]{2,1,0:T(8,128)(2,1)} %bitcast.7) | data formatting | bytes 2097152

commit v4 on v3

v4 whole, which is shorter than its diff:
```python
import jax
import jax.numpy as jnp
from jax import lax
from jax.experimental import pallas as pl
from jax.experimental.pallas import tpu as pltpu
from jax.sharding import PartitionSpec as P

MESH = pl.DeviceIdType.MESH
BF16 = jnp.bfloat16
F32 = jnp.float32


def turned(x):
    wide = pltpu.roll(x.astype(F32), 64, x.ndim - 1)
    lane = lax.broadcasted_iota(jnp.int32, wide.shape, wide.ndim - 1)
    return jnp.where(lane < 64, -wide, wide).astype(BF16)


def dot(a, b):
    return jnp.dot(a, b, preferred_element_type=F32).astype(BF16)


def mixed(own, partner, transfer):
    operand = jnp.concatenate([own, turned(own), partner, turned(partner)], axis=0)
    return dot(transfer, operand)


def mixed_pair(a, b, transfer_a, transfer_b):
    ta, tb = turned(a), turned(b)
    out_a = dot(transfer_a, jnp.concatenate([a, ta, b, tb], axis=0))
    out_b = dot(transfer_b, jnp.concatenate([b, tb, a, ta], axis=0))
    return out_a, out_b


def paired(values, bit, transfer):
    result = [None] * len(values)
    for n in range(len(values)):
        if n & bit == 0:
            m = n | bit
            result[n], result[m] = mixed_pair(values[n], values[m], transfer(n), transfer(m))
    return result


NH = 4
CH = 8 // NH


def kernel(
    src, leaf, st, tt, out,
    src_v, leaf_v, s0, sb, sq, t01, t23, c0, c0p, c1, cb, yk, ys, yp, wm, mb, rb,
    load_sem, own_sem, s_recv, s3_recv, t_recv, p_recv, y_recv, z_recv, m_recv, r_recv, sent,
):
    x = lax.axis_index("gx")
    g = lax.axis_index("gy")
    z = g // 8
    z1 = z // 2
    z0 = z % 2
    a = (z0 + z1) % 2
    other = 1 - a
    yc = g % 8
    core = g % 2
    mate = z + 1 - 2 * z0

    def z_of(a_bit, k):
        return 2 * k + (a_bit + k) % 2

    def remote(source, target, send, recv, device):
        return pltpu.make_async_remote_copy(
            src_ref=source,
            dst_ref=target,
            send_sem=sent.at[send],
            recv_sem=recv,
            device_id=device,
            device_id_type=MESH,
        )

    def drain(ref, sem):
        pltpu.make_async_copy(ref, ref, sem).wait()

    def s_copy(k, r):
        to = (yc + r) % 8
        return remote(
            st.at[pl.ds(1, 2), :, k, :, to], sb.at[:, yc, k], 0, s_recv.at[k], (x, z * 8 + to)
        )

    def s3_copy(far, k, r):
        to = (yc + r) % 8
        return remote(
            st.at[3, :, k, ((other if far else a) + k) % 2, to],
            sq.at[8 * far + yc, k],
            1,
            s3_recv.at[k],
            (x, (mate if far else z) * 8 + to),
        )

    def t01_copy(i, h):
        to_x = (x + i) % 4
        to_z1 = (z1 + h) % 2
        return remote(
            tt.at[pl.ds(0, 2), to_x, to_z1],
            t01.at[:, 2 * x + z1],
            2,
            t_recv.at[0],
            (to_x, z_of(a, to_z1) * 8 + yc),
        )

    def t23_copy(level, j):
        to_z = (z + j) % 4
        return remote(
            tt.at[level + 2, :, to_z // 2, to_z % 2],
            t23.at[level, z],
            3,
            t_recv.at[1 + level],
            (x, to_z * 8 + yc),
        )

    def p_copy(k):
        return remote(c0.at[k], c0p.at[k], 4, p_recv.at[k], (x, g + 1 - 2 * core))

    def y_copy(k, r):
        to = (yc + r) % 8
        return remote(c1.at[to, k], cb.at[yc, k], 5, y_recv.at[k], (x, z * 8 + to))

    def z_copy(k, q):
        chunk = pl.ds(CH * q, CH)
        return remote(
            ys.at[k, chunk], yp.at[k, chunk], 6, z_recv.at[k, q], (x, mate * 8 + yc)
        )

    def m_copy(k, q, i, h):
        chunk = pl.ds(CH * q, CH)
        to_x = (x + i) % 4
        to_z0 = (z0 + h) % 2
        return remote(
            wm.at[to_z0, to_x, k, chunk],
            mb.at[2 * x + a, k, chunk],
            7,
            m_recv.at[q],
            (to_x, (2 * z1 + to_z0) * 8 + yc),
        )

    def r_copy(q, j):
        chunk = pl.ds(CH * q, CH)
        to_z = (z + j) % 4
        return remote(
            rb.at[to_z, :, chunk], out.at[:, z, chunk], 8, r_recv, (x, to_z * 8 + yc)
        )

    near = [(i, h) for h in range(2) for i in (1, 3, 2, 0) if (i, h) != (0, 0)]
    along_y = [2, 6, 4, 1, 3, 7, 5]
    along_z = [1, 3, 2]
    s3_sent = [(far, r) for r in [0] + along_y for far in (0, 1) if (far, r) != (0, 0)]

    loads = [
        pltpu.make_async_copy(src, src_v, load_sem.at[0]),
        pltpu.make_async_copy(leaf, leaf_v, load_sem.at[1]),
        pltpu.make_async_copy(st.at[0], s0, load_sem.at[2]),
    ]
    for copy in loads:
        copy.start()
    own_s = [
        pltpu.make_async_copy(st.at[pl.ds(1, 2), :, k, :, yc], sb.at[:, yc, k], own_sem.at[k])
        for k in range(2)
    ]
    own_s3 = [
        pltpu.make_async_copy(st.at[3, :, k, (a + k) % 2, yc], sq.at[yc, k], own_sem.at[2 + k])
        for k in range(2)
    ]
    own_t01 = pltpu.make_async_copy(tt.at[pl.ds(0, 2), x, z1], t01.at[:, 2 * x + z1], own_sem.at[4])
    own_t23 = pltpu.make_async_copy(tt.at[pl.ds(2, 2), :, z1, z0], t23.at[:, z], own_sem.at[5])
    for copy in own_s + own_s3 + [own_t01, own_t23]:
        copy.start()

    barrier = pltpu.get_barrier_semaphore()
    peers = [(x, z * 8 + (yc + r) % 8) for r in range(1, 8)]
    peers += [(x, mate * 8 + (yc + r) % 8) for r in range(8)]
    peers += [(x, ((z + 2) % 4) * 8 + yc), (x, ((mate + 2) % 4) * 8 + yc)]
    for i in range(1, 4):
        for to_z in (z, mate, z_of(a, 1 - z1)):
            peers.append(((x + i) % 4, to_z * 8 + yc))
    for peer in peers:
        pl.semaphore_signal(barrier, inc=1, device_id=peer, device_id_type=MESH)

    loads[0].wait()
    loads[1].wait()

    def leaf_body(n, carry):
        vx, k, j = n // 4, n // 2 % 2, n % 2
        for i in range(8):
            v = src_v[vx, k, j, i]
            c0[k, vx, j, i] = dot(leaf_v[vx, k, j, i], jnp.concatenate([v, turned(v)], axis=0))
        return carry

    lax.fori_loop(0, 16, leaf_body, 0)
    pl.semaphore_wait(barrier, len(peers))

    for k in range(2):
        p_copy(k).start()
    for r in along_y:
        s_copy(0, r).start()
    for i, h in near:
        t01_copy(i, h).start()
    for j in along_z:
        t23_copy(0, j).start()

    loads[2].wait()
    for k in range(2):
        p_copy(k).wait_recv()

        def first_body(vx, carry, k=k):
            for j in range(2):
                for i in range(8):
                    c1[i, k, vx, j] = mixed(c0[k, vx, j, i], c0p[k, vx, j, i], s0[vx, k, j, i])
            return carry

        lax.fori_loop(0, 4, first_body, 0)
        if k == 1:
            for r in along_y:
                s_copy(1, r).start()
        for r in along_y:
            y_copy(k, r).start()
        for far, r in s3_sent:
            s3_copy(far, k, r).start()
        cb[yc, k] = c1[yc, k]

    for k in range(2):
        own_s[k].wait()
        drain(sb.at[:, pl.ds(0, 7), k], s_recv.at[k])
        drain(cb.at[pl.ds(0, 7), k], y_recv.at[k])

        def y_body(vx, carry, k=k):
            for target, a_bit in ((ys, other), (yk, a)):
                j = (a_bit + k) % 2
                values = [cb[i, k, vx, j] for i in range(8)]
                for level, bit in enumerate((2, 4)):
                    values = paired(values, bit, lambda i: sb[level, i, k, vx, j])
                for i in range(8):
                    target[k, i, vx] = values[i]
            return carry

        lax.fori_loop(0, 4, y_body, 0)
        for q in range(NH):
            z_copy(k, q).start()
        if k == 0:
            for j in along_z:
                t23_copy(1, j).start()

        own_s3[k].wait()
        drain(sq.at[pl.ds(0, 15), k], s3_recv.at[k])
        if k == 0:
            own_t01.wait()
            drain(t01.at[:, pl.ds(0, 7)], t_recv.at[0])

        sides = (z0, 1 - z0)

        def x_body(q, carry, k=k):
            z_copy(k, q).wait_recv()
            for b in range(CH):
                i = CH * q + b
                values = [yk[k, i, n] for n in range(4)] + [yp[k, i, n] for n in range(4)]
                values = paired(values, 4, lambda n: sq[8 * (n // 4) + i, k, n % 4])
                for level, bit in enumerate((2, 1)):
                    values = paired(
                        values, bit, lambda n: t01[level, 2 * (n % 4) + k, sides[n // 4], i]
                    )
                for n in range(8):
                    wm[sides[n // 4], n % 4, k, i] = values[n]
            for i, h in near:
                m_copy(k, q, i, h).start()
            chunk = pl.ds(CH * q, CH)
            mb[2 * x + a, k, chunk] = wm[z0, x, k, chunk]
            return carry

        lax.fori_loop(0, NH, x_body, 0)

    own_t23.wait()
    for level in range(2):
        drain(t23.at[level, pl.ds(0, 3)], t_recv.at[1 + level])

    def last_body(q, carry):
        drain(mb.at[pl.ds(0, 7), :, pl.ds(CH * q, CH)], m_recv.at[q])
        for b in range(CH):
            i = CH * q + b
            for n in range(4):
                values = [mb[2 * n + m // 2, m % 2, i] for m in range(4)]
                for level, bit in enumerate((3, 2)):
                    result = [None] * 4
                    for m in range(2):
                        w = m ^ bit
                        result[m], result[w] = mixed_pair(
                            values[m],
                            values[w],
                            t23[level, z_of(m // 2, m % 2), n, i],
                            t23[level, z_of(w // 2, w % 2), n, i],
                        )
                    values = result
                for m in range(4):
                    rb[z_of(m // 2, m % 2), n, i] = values[m]
        for j in along_z:
            r_copy(q, j).start()
        chunk = pl.ds(CH * q, CH)
        out[:, z, chunk] = rb[z, :, chunk]
        return carry

    lax.fori_loop(0, NH, last_body, 0)

    drain(out.at[:, pl.ds(0, 3)], r_recv)
    drain(sb.at[:, pl.ds(0, 7)], sent.at[0])
    drain(sq.at[pl.ds(0, 15)], sent.at[1])
    drain(t01.at[:, pl.ds(0, 7)], sent.at[2])
    drain(t23.at[:, pl.ds(0, 3)], sent.at[3])
    drain(c0, sent.at[4])
    drain(cb.at[pl.ds(0, 7)], sent.at[5])
    drain(ys, sent.at[6])
    drain(mb.at[pl.ds(0, 7)], sent.at[7])
    drain(out.at[:, pl.ds(0, 3)], sent.at[8])


def local(source_values, leaf_maps, source_transfers, target_transfers):
    dma = pltpu.SemaphoreType.DMA
    box = (32, 128)

    def vmem(*shape):
        return pltpu.VMEM(shape + box, BF16)

    out = pl.pallas_call(
        kernel,
        out_shape=jax.ShapeDtypeStruct((4, 4, 8) + box, BF16),
        in_specs=[pl.BlockSpec(memory_space=pl.ANY)] * 4,
        out_specs=pl.BlockSpec(memory_space=pltpu.VMEM),
        scratch_shapes=[
            pltpu.VMEM((4, 2, 2, 8, 64, 128), BF16),
            vmem(4, 2, 2, 8),
            vmem(4, 2, 2, 8),
            vmem(2, 8, 2, 4, 2),
            vmem(16, 2, 4),
            vmem(2, 8, 2, 8),
            vmem(2, 4, 4, 8),
            vmem(2, 4, 2, 8),
            vmem(2, 4, 2, 8),
            vmem(8, 2, 4, 2),
            vmem(8, 2, 4, 2),
            vmem(2, 8, 4),
            vmem(2, 8, 4),
            vmem(2, 8, 4),
            vmem(2, 4, 2, 8),
            vmem(8, 2, 8),
            vmem(4, 4, 8),
            dma((3,)),
            dma((6,)),
            dma((2,)),
            dma((2,)),
            dma((3,)),
            dma((2,)),
            dma((2,)),
            dma((2, NH)),
            dma((NH,)),
            dma,
            dma((9,)),
        ],
        compiler_params=pltpu.CompilerParams(
            collective_id=0, has_side_effects=True, vmem_limit_bytes=54000 * 1024
        ),
    )(
        source_values.reshape(4, 2, 2, 8, 64, 128),
        leaf_maps.reshape((4, 2, 2, 8) + box),
        source_transfers.reshape((4, 4, 2, 2, 8) + box),
        target_transfers.reshape((4, 4, 2, 2, 8) + box),
    )
    return out.reshape((128,) + box)


def solution(mesh):
    return jax.shard_map(
        local,
        mesh=mesh,
        in_specs=(
            P(("gx", "gy"), None, None),
            P(("gx", "gy"), None, None),
            P(None, ("gx", "gy"), None, None),
            P(None, ("gx", "gy"), None, None),
        ),
        out_specs=P(("gx", "gy"), None, None),
        check_vma=False,
    )
```

time: 99.2 us -> 89 us (0.90)
  the two profiles are of different devices: /device:TPU:4 before, /device:TPU:1 now
where the time goes in v4:
time: 89 us; the launch traced here: 88.9 us
  Pallas kernels  88 us (99%)
  local copies, waits for them, and re-layouts  0.97 us (1%)
    pallas_call x1, Pallas kernels, local(): pl.pallas_call(kernel, out_shape=jax.ShapeDtypeStruct((4, 4, 8) + box, BF...  88 us

profile of v4, /device:TPU:1, one launch (start us, length us, event | category | flops | bytes accessed | tf_op | source)
XLA Modules:
  0.0 88.9 jit_solution(5793608100299727375)
XLA Ops:
  0.0 88.0 %shard_map.46 = bf16[4,4,8,32,128]{4,3,2,1,0:T(8,128)(2,1)S(1)} custom-call(bf16[4,2,2,8,64,128]{5,4,3,2,1,0:T(8,128)(2,1)} %bitcast.8, bf16[4,2,2,8,32,128]{5,4,3,2,1,0:T(8,128)(2,1)} %bitcast.9, bf16[4,4,2,2,8,32,128]{6,5,4,3,2,1,0:T(8,128)(2,1)} %bitcast.6, bf16[4,4,2,2,8,32,128]{6,5,4,3,2,1,0:T(8,128)(2,1)} %bitcast.7), custom_call_target="tpu_custom_call" | custom-call | tf_op jit(solution)/shard_map/pallas_call | solution.py:326
  88.0 1.0 %copy.6 = bf16[128,32,128]{2,1,0:T(8,128)(2,1)} copy(bf16[128,32,128]{2,1,0:T(8,128)(2,1)S(1)} %bitcast.5) | data formatting | bytes 2097152

commit v5 on v4

--- a/solution.py
+++ b/solution.py
@@ -11,9 +11,8 @@
 
 
 def turned(x):
-    wide = pltpu.roll(x.astype(F32), 64, x.ndim - 1)
-    lane = lax.broadcasted_iota(jnp.int32, wide.shape, wide.ndim - 1)
-    return jnp.where(lane < 64, -wide, wide).astype(BF16)
+    lane = lax.broadcasted_iota(jnp.int32, (1, 128), 1)
+    return pltpu.roll(x, 64, 1) * jnp.where(lane < 64, -1.0, 1.0).astype(BF16)
 
 
 def dot(a, b):
@@ -26,23 +25,23 @@
 
 
 def mixed_pair(a, b, transfer_a, transfer_b):
-    ta, tb = turned(a), turned(b)
-    out_a = dot(transfer_a, jnp.concatenate([a, ta, b, tb], axis=0))
-    out_b = dot(transfer_b, jnp.concatenate([b, tb, a, ta], axis=0))
-    return out_a, out_b
+    operand = jnp.concatenate([a, turned(a), b, turned(b)], axis=0)
+    out = dot(jnp.concatenate([transfer_a, pltpu.roll(transfer_b, 64, 1)], axis=0), operand)
+    return out[:32], out[32:]
 
 
 def paired(values, bit, transfer):
     result = [None] * len(values)
     for n in range(len(values)):
-        if n & bit == 0:
-            m = n | bit
+        if n < n ^ bit:
+            m = n ^ bit
             result[n], result[m] = mixed_pair(values[n], values[m], transfer(n), transfer(m))
     return result
 
 
 NH = 4
 CH = 8 // NH
+LAG = 2
 
 
 def kernel(
@@ -104,8 +103,7 @@
             (to_x, z_of(a, to_z1) * 8 + yc),
         )
 
-    def t23_copy(level, j):
-        to_z = (z + j) % 4
+    def t23_copy(level, to_z):
         return remote(
             tt.at[level + 2, :, to_z // 2, to_z % 2],
             t23.at[level, z],
@@ -181,128 +179,144 @@
     for peer in peers:
         pl.semaphore_signal(barrier, inc=1, device_id=peer, device_id_type=MESH)
 
-    loads[0].wait()
-    loads[1].wait()
-
-    def leaf_body(n, carry):
-        vx, k, j = n // 4, n // 2 % 2, n % 2
-        for i in range(8):
-            v = src_v[vx, k, j, i]
-            c0[k, vx, j, i] = dot(leaf_v[vx, k, j, i], jnp.concatenate([v, turned(v)], axis=0))
-        return carry
-
-    lax.fori_loop(0, 16, leaf_body, 0)
     pl.semaphore_wait(barrier, len(peers))
-
-    for k in range(2):
-        p_copy(k).start()
     for r in along_y:
         s_copy(0, r).start()
     for i, h in near:
         t01_copy(i, h).start()
-    for j in along_z:
-        t23_copy(0, j).start()
+    for to_z in (mate, (z + 2) % 4, (mate + 2) % 4):
+        t23_copy(0, to_z).start()
+
+    loads[0].wait()
+    loads[1].wait()
+    for k in range(2):
+
+        def leaf_body(n, carry, k=k):
+            for w in range(4):
+                vx, j = 2 * n + w // 2, w % 2
+                for i in range(8):
+                    v = src_v[vx, k, j, i]
+                    c0[k, vx, j, i] = dot(
+                        leaf_v[vx, k, j, i], jnp.concatenate([v, turned(v)], axis=0)
+                    )
+            return carry
+
+        lax.fori_loop(0, 2, leaf_body, 0)
+        p_copy(k).start()
 
     loads[2].wait()
     for k in range(2):
         p_copy(k).wait_recv()
 
-        def first_body(vx, carry, k=k):
-            for j in range(2):
+        def first_body(n, carry, k=k):
+            for w in range(4):
+                vx, j = 2 * n + w // 2, w % 2
                 for i in range(8):
                     c1[i, k, vx, j] = mixed(c0[k, vx, j, i], c0p[k, vx, j, i], s0[vx, k, j, i])
             return carry
 
-        lax.fori_loop(0, 4, first_body, 0)
-        if k == 1:
+        lax.fori_loop(0, 2, first_body, 0)
+        for r in along_y:
+            y_copy(k, r).start()
+        if k == 0:
+            for far, r in s3_sent:
+                s3_copy(far, 0, r).start()
+            for to_z in (mate, (z + 2) % 4, (mate + 2) % 4):
+                t23_copy(1, to_z).start()
             for r in along_y:
                 s_copy(1, r).start()
-        for r in along_y:
-            y_copy(k, r).start()
-        for far, r in s3_sent:
-            s3_copy(far, k, r).start()
         cb[yc, k] = c1[yc, k]
+
+    sides = (z0, 1 - z0)
+
+    def x_stage(k, q):
+        z_copy(k, q).wait_recv()
+
+        rows = [CH * q + b for b in range(CH)]
+        values = [v for i in rows for m in (yk, yp) for v in [m[k, i, n] for n in range(4)]]
+        values = paired(
+            values, 4, lambda n: sq[8 * (n // 4 % 2) + rows[n // 8], k, n % 4]
+        )
+        for level, bit in enumerate((2, 1)):
+            values = paired(
+                values,
+                bit,
+                lambda n: t01[level, 2 * (n % 4) + k, sides[n // 4 % 2], rows[n // 8]],
+            )
+        for n in range(8 * CH):
+            wm[sides[n // 4 % 2], n % 4, k, rows[n // 8]] = values[n]
+        for i, h in near:
+            m_copy(k, q, i, h).start()
+        chunk = pl.ds(CH * q, CH)
+        mb[2 * x + a, k, chunk] = wm[z0, x, k, chunk]
+
+    def last_stage(q):
+        drain(mb.at[pl.ds(0, 7), :, pl.ds(CH * q, CH)], m_recv.at[q])
+
+        places = [(CH * q + b, n) for b in range(CH) for n in range(4)]
+        values = [mb[2 * n + m // 2, m % 2, i] for i, n in places for m in range(4)]
+        for level, bit in enumerate((3, 2)):
+            values = paired(
+                values,
+                bit,
+                lambda w: t23[
+                    level, z_of(w % 4 // 2, w % 2), places[w // 4][1], places[w // 4][0]
+                ],
+            )
+        for w in range(len(values)):
+            rb[z_of(w % 4 // 2, w % 2), places[w // 4][1], places[w // 4][0]] = values[w]
+        for j in along_z:
+            r_copy(q, j).start()
+        chunk = pl.ds(CH * q, CH)
+        out[:, z, chunk] = rb[z, :, chunk]
 
     for k in range(2):
         own_s[k].wait()
         drain(sb.at[:, pl.ds(0, 7), k], s_recv.at[k])
         drain(cb.at[pl.ds(0, 7), k], y_recv.at[k])
 
-        def y_body(vx, carry, k=k):
-            for target, a_bit in ((ys, other), (yk, a)):
-                j = (a_bit + k) % 2
-                values = [cb[i, k, vx, j] for i in range(8)]
-                for level, bit in enumerate((2, 4)):
-                    values = paired(values, bit, lambda i: sb[level, i, k, vx, j])
-                for i in range(8):
-                    target[k, i, vx] = values[i]
+        def y_body(h, carry, k=k):
+            columns = [
+                (2 * h + n, target, (a_bit + k) % 2)
+                for n in range(2)
+                for target, a_bit in ((ys, other), (yk, a))
+            ]
+            values = [cb[i, k, vx, j] for vx, _, j in columns for i in range(8)]
+            for level, bit in enumerate((2, 4)):
+                values = paired(
+                    values,
+                    bit,
+                    lambda n: sb[level, n % 8, k, columns[n // 8][0], columns[n // 8][2]],
+                )
+            for n in range(32):
+                vx, target, _ = columns[n // 8]
+                target[k, n % 8, vx] = values[n]
             return carry
 
-        lax.fori_loop(0, 4, y_body, 0)
+        lax.fori_loop(0, 2, y_body, 0)
         for q in range(NH):
             z_copy(k, q).start()
         if k == 0:
-            for j in along_z:
-                t23_copy(1, j).start()
+            for far, r in s3_sent:
+                s3_copy(far, 1, r).start()
 
         own_s3[k].wait()
         drain(sq.at[pl.ds(0, 15), k], s3_recv.at[k])
         if k == 0:
             own_t01.wait()
             drain(t01.at[:, pl.ds(0, 7)], t_recv.at[0])
-
-        sides = (z0, 1 - z0)
-
-        def x_body(q, carry, k=k):
-            z_copy(k, q).wait_recv()
-            for b in range(CH):
-                i = CH * q + b
-                values = [yk[k, i, n] for n in range(4)] + [yp[k, i, n] for n in range(4)]
-                values = paired(values, 4, lambda n: sq[8 * (n // 4) + i, k, n % 4])
-                for level, bit in enumerate((2, 1)):
-                    values = paired(
-                        values, bit, lambda n: t01[level, 2 * (n % 4) + k, sides[n // 4], i]
-                    )
-                for n in range(8):
-                    wm[sides[n // 4], n % 4, k, i] = values[n]
-            for i, h in near:
-                m_copy(k, q, i, h).start()
-            chunk = pl.ds(CH * q, CH)
-            mb[2 * x + a, k, chunk] = wm[z0, x, k, chunk]
-            return carry
-
-        lax.fori_loop(0, NH, x_body, 0)
+            for q in range(NH):
+                x_stage(0, q)
 
     own_t23.wait()
-    for level in range(2):
-        drain(t23.at[level, pl.ds(0, 3)], t_recv.at[1 + level])
-
-    def last_body(q, carry):
-        drain(mb.at[pl.ds(0, 7), :, pl.ds(CH * q, CH)], m_recv.at[q])
-        for b in range(CH):
-            i = CH * q + b
-            for n in range(4):
-                values = [mb[2 * n + m // 2, m % 2, i] for m in range(4)]
-                for level, bit in enumerate((3, 2)):
-                    result = [None] * 4
-                    for m in range(2):
-                        w = m ^ bit
-                        result[m], result[w] = mixed_pair(
-                            values[m],
-                            values[w],
-                            t23[level, z_of(m // 2, m % 2), n, i],
-                            t23[level, z_of(w // 2, w % 2), n, i],
-                        )
-                    values = result
-                for m in range(4):
-                    rb[z_of(m // 2, m % 2), n, i] = values[m]
-        for j in along_z:
-            r_copy(q, j).start()
-        chunk = pl.ds(CH * q, CH)
-        out[:, z, chunk] = rb[z, :, chunk]
-        return carry
-
-    lax.fori_loop(0, NH, last_body, 0)
+    for q in range(NH + LAG):
+        if q < NH:
+            x_stage(1, q)
+        if q == LAG:
+            for level in range(2):
+                drain(t23.at[level, pl.ds(0, 3)], t_recv.at[1 + level])
+        if q >= LAG:
+            last_stage(q - LAG)
 
     drain(out.at[:, pl.ds(0, 3)], r_recv)
     drain(sb.at[:, pl.ds(0, 7)], sent.at[0])

time: 89 us -> 84 us (0.944)
  the two profiles are of different devices: /device:TPU:1 before, /device:TPU:4 now
where the time goes in v5:
time: 84 us; the launch traced here: 83.6 us
  Pallas kernels  82.7 us (98%)
  local copies, waits for them, and re-layouts  0.97 us (1%)
    pallas_call x1, Pallas kernels, local(): pl.pallas_call(kernel, out_shape=jax.ShapeDtypeStruct((4, 4, 8) + box, BF...  82.7 us

profile of v5, /device:TPU:4, one launch (start us, length us, event | category | flops | bytes accessed | tf_op | source)
XLA Modules:
  0.0 83.6 jit_solution(5724985535168061976)
XLA Ops:
  0.0 82.7 %shard_map.46 = bf16[4,4,8,32,128]{4,3,2,1,0:T(8,128)(2,1)S(1)} custom-call(bf16[4,2,2,8,64,128]{5,4,3,2,1,0:T(8,128)(2,1)} %bitcast.8, bf16[4,2,2,8,32,128]{5,4,3,2,1,0:T(8,128)(2,1)} %bitcast.9, bf16[4,4,2,2,8,32,128]{6,5,4,3,2,1,0:T(8,128)(2,1)} %bitcast.6, bf16[4,4,2,2,8,32,128]{6,5,4,3,2,1,0:T(8,128)(2,1)} %bitcast.7), custom_call_target="tpu_custom_call" | custom-call | tf_op jit(solution)/shard_map/pallas_call | solution.py:340
  82.7 1.0 %copy.6 = bf16[128,32,128]{2,1,0:T(8,128)(2,1)} copy(bf16[128,32,128]{2,1,0:T(8,128)(2,1)S(1)} %bitcast.5) | data formatting | bytes 2097152

commit v6 on v5

--- a/solution.py
+++ b/solution.py
@@ -46,8 +46,8 @@
 
 def kernel(
     src, leaf, st, tt, out,
-    src_v, leaf_v, s0, sb, sq, t01, t23, c0, c0p, c1, cb, yk, ys, yp, wm, mb, rb,
-    load_sem, own_sem, s_recv, s3_recv, t_recv, p_recv, y_recv, z_recv, m_recv, r_recv, sent,
+    src_v, leaf_v, s0, sb, sq, z3, t01, t23, c0, c0p, c1, cb, yk, ys, yp, wm, mb, rb,
+    load_sem, own_sem, s_recv, s3_recv, z3_recv, t_recv, p_recv, y_recv, z_recv, m_recv, r_recv, sent,
 ):
     x = lax.axis_index("gx")
     g = lax.axis_index("gy")
@@ -82,14 +82,21 @@
             st.at[pl.ds(1, 2), :, k, :, to], sb.at[:, yc, k], 0, s_recv.at[k], (x, z * 8 + to)
         )
 
-    def s3_copy(far, k, r):
+    def s3_copy(k, r):
         to = (yc + r) % 8
         return remote(
-            st.at[3, :, k, ((other if far else a) + k) % 2, to],
-            sq.at[8 * far + yc, k],
-            1,
-            s3_recv.at[k],
-            (x, (mate if far else z) * 8 + to),
+            st.at[3, :, k, (a + k) % 2, to], sq.at[yc, k], 1, s3_recv.at[k], (x, z * 8 + to)
+        )
+
+    def cross_copy(k):
+        return remote(
+            st.at[3, :, k, (other + k) % 2], z3.at[k], 9, z3_recv.at[k], (x, mate * 8 + yc)
+        )
+
+    def pass_copy(k, r):
+        to = (yc + r) % 8
+        return remote(
+            z3.at[k, :, to], sq.at[8 + yc, k], 1, s3_recv.at[k], (x, z * 8 + to)
         )
 
     def t01_copy(i, h):
@@ -147,7 +154,6 @@
     near = [(i, h) for h in range(2) for i in (1, 3, 2, 0) if (i, h) != (0, 0)]
     along_y = [2, 6, 4, 1, 3, 7, 5]
     along_z = [1, 3, 2]
-    s3_sent = [(far, r) for r in [0] + along_y for far in (0, 1) if (far, r) != (0, 0)]
 
     loads = [
         pltpu.make_async_copy(src, src_v, load_sem.at[0]),
@@ -171,8 +177,7 @@
 
     barrier = pltpu.get_barrier_semaphore()
     peers = [(x, z * 8 + (yc + r) % 8) for r in range(1, 8)]
-    peers += [(x, mate * 8 + (yc + r) % 8) for r in range(8)]
-    peers += [(x, ((z + 2) % 4) * 8 + yc), (x, ((mate + 2) % 4) * 8 + yc)]
+    peers += [(x, ((z + j) % 4) * 8 + yc) for j in range(1, 4)]
     for i in range(1, 4):
         for to_z in (z, mate, z_of(a, 1 - z1)):
             peers.append(((x + i) % 4, to_z * 8 + yc))
@@ -182,10 +187,12 @@
     pl.semaphore_wait(barrier, len(peers))
     for r in along_y:
         s_copy(0, r).start()
+    for k in range(2):
+        cross_copy(k).start()
     for i, h in near:
         t01_copy(i, h).start()
-    for to_z in (mate, (z + 2) % 4, (mate + 2) % 4):
-        t23_copy(0, to_z).start()
+    for level in range(2):
+        t23_copy(level, mate).start()
 
     loads[0].wait()
     loads[1].wait()
@@ -204,6 +211,14 @@
         lax.fori_loop(0, 2, leaf_body, 0)
         p_copy(k).start()
 
+    def last_source(k):
+        for r in along_y:
+            s3_copy(k, r).start()
+        drain(z3.at[k], z3_recv.at[k])
+        for r in along_y:
+            pass_copy(k, r).start()
+        sq[8 + yc, k] = z3[k, :, yc]
+
     loads[2].wait()
     for k in range(2):
         p_copy(k).wait_recv()
@@ -219,10 +234,7 @@
         for r in along_y:
             y_copy(k, r).start()
         if k == 0:
-            for far, r in s3_sent:
-                s3_copy(far, 0, r).start()
-            for to_z in (mate, (z + 2) % 4, (mate + 2) % 4):
-                t23_copy(1, to_z).start()
+            last_source(0)
             for r in along_y:
                 s_copy(1, r).start()
         cb[yc, k] = c1[yc, k]
@@ -297,11 +309,13 @@
         for q in range(NH):
             z_copy(k, q).start()
         if k == 0:
-            for far, r in s3_sent:
-                s3_copy(far, 1, r).start()
+            for to_z in ((z + 2) % 4, (mate + 2) % 4):
+                for level in range(2):
+                    t23_copy(level, to_z).start()
+            last_source(1)
 
         own_s3[k].wait()
-        drain(sq.at[pl.ds(0, 15), k], s3_recv.at[k])
+        drain(sq.at[pl.ds(0, 14), k], s3_recv.at[k])
         if k == 0:
             own_t01.wait()
             drain(t01.at[:, pl.ds(0, 7)], t_recv.at[0])
@@ -320,7 +334,8 @@
 
     drain(out.at[:, pl.ds(0, 3)], r_recv)
     drain(sb.at[:, pl.ds(0, 7)], sent.at[0])
-    drain(sq.at[pl.ds(0, 15)], sent.at[1])
+    drain(sq.at[pl.ds(0, 14)], sent.at[1])
+    drain(z3, sent.at[9])
     drain(t01.at[:, pl.ds(0, 7)], sent.at[2])
     drain(t23.at[:, pl.ds(0, 3)], sent.at[3])
     drain(c0, sent.at[4])
@@ -348,6 +363,7 @@
             vmem(4, 2, 2, 8),
             vmem(2, 8, 2, 4, 2),
             vmem(16, 2, 4),
+            vmem(2, 4, 8),
             vmem(2, 8, 2, 8),
             vmem(2, 4, 4, 8),
             vmem(2, 4, 2, 8),
@@ -364,13 +380,14 @@
             dma((6,)),
             dma((2,)),
             dma((2,)),
+            dma((2,)),
             dma((3,)),
             dma((2,)),
             dma((2,)),
             dma((2, NH)),
             dma((NH,)),
             dma,
-            dma((9,)),
+            dma((10,)),
         ],
         compiler_params=pltpu.CompilerParams(
             collective_id=0, has_side_effects=True, vmem_limit_bytes=54000 * 1024

time: 84 us -> 80.1 us (0.954); the launches traced: 83.6 us -> 78.8 us
  Pallas kernels: 82.7 us -> 77.8 us
    pallas_call x1, Pallas kernels: 82.7 us -> 77.8 us  [local(): pl.pallas_call(kernel, out_shape=jax.ShapeDtypeStruct((4, 4, 8) + box, BF...]
where the time goes in v6:
time: 80.1 us; the launch traced here: 78.8 us
  Pallas kernels  77.8 us (97%)
  local copies, waits for them, and re-layouts  0.97 us (1%)
    pallas_call x1, Pallas kernels, local(): pl.pallas_call(kernel, out_shape=jax.ShapeDtypeStruct((4, 4, 8) + box, BF...  77.8 us

profile of v6, /device:TPU:4, one launch (start us, length us, event | category | flops | bytes accessed | tf_op | source)
XLA Modules:
  0.0 78.8 jit_solution(8636013401413191902)
XLA Ops:
  0.0 77.8 %shard_map.46 = bf16[4,4,8,32,128]{4,3,2,1,0:T(8,128)(2,1)S(1)} custom-call(bf16[4,2,2,8,64,128]{5,4,3,2,1,0:T(8,128)(2,1)} %bitcast.8, bf16[4,2,2,8,32,128]{5,4,3,2,1,0:T(8,128)(2,1)} %bitcast.9, bf16[4,4,2,2,8,32,128]{6,5,4,3,2,1,0:T(8,128)(2,1)} %bitcast.6, bf16[4,4,2,2,8,32,128]{6,5,4,3,2,1,0:T(8,128)(2,1)} %bitcast.7), custom_call_target="tpu_custom_call" | custom-call | tf_op jit(solution)/shard_map/pallas_call | solution.py:355
  77.8 1.0 %copy.6 = bf16[128,32,128]{2,1,0:T(8,128)(2,1)} copy(bf16[128,32,128]{2,1,0:T(8,128)(2,1)S(1)} %bitcast.5) | data formatting | bytes 2097152

commit v7 on v6

--- a/solution.py
+++ b/solution.py
@@ -39,9 +39,9 @@
     return result
 
 
-NH = 4
+NH = 8
 CH = 8 // NH
-LAG = 2
+LAG = 6
 
 
 def kernel(
@@ -144,16 +144,15 @@
             (to_x, (2 * z1 + to_z0) * 8 + yc),
         )
 
-    def r_copy(q, j):
+    def r_copy(q, to_z):
         chunk = pl.ds(CH * q, CH)
-        to_z = (z + j) % 4
         return remote(
             rb.at[to_z, :, chunk], out.at[:, z, chunk], 8, r_recv, (x, to_z * 8 + yc)
         )
 
     near = [(i, h) for h in range(2) for i in (1, 3, 2, 0) if (i, h) != (0, 0)]
     along_y = [2, 6, 4, 1, 3, 7, 5]
-    along_z = [1, 3, 2]
+    along_z = [mate, (z + 2) % 4, (mate + 2) % 4]
 
     loads = [
         pltpu.make_async_copy(src, src_v, load_sem.at[0]),
@@ -277,8 +276,8 @@
             )
         for w in range(len(values)):
             rb[z_of(w % 4 // 2, w % 2), places[w // 4][1], places[w // 4][0]] = values[w]
-        for j in along_z:
-            r_copy(q, j).start()
+        for to_z in along_z:
+            r_copy(q, to_z).start()
         chunk = pl.ds(CH * q, CH)
         out[:, z, chunk] = rb[z, :, chunk]
 
@@ -309,10 +308,10 @@
         for q in range(NH):
             z_copy(k, q).start()
         if k == 0:
-            for to_z in ((z + 2) % 4, (mate + 2) % 4):
-                for level in range(2):
+            last_source(1)
+            for level in range(2):
+                for to_z in along_z[1:]:
                     t23_copy(level, to_z).start()
-            last_source(1)
 
         own_s3[k].wait()
         drain(sq.at[pl.ds(0, 14), k], s3_recv.at[k])

time: 80.1 us -> 78.9 us (0.985); the launches traced: 78.8 us -> 78.6 us
  no operation moved by 1% of the time
where the time goes in v7:
time: 78.9 us; the launch traced here: 78.6 us
  Pallas kernels  77.6 us (98%)
  local copies, waits for them, and re-layouts  0.97 us (1%)
    pallas_call x1, Pallas kernels, local(): pl.pallas_call(kernel, out_shape=jax.ShapeDtypeStruct((4, 4, 8) + box, BF...  77.6 us

profile of v7, /device:TPU:4, one launch (start us, length us, event | category | flops | bytes accessed | tf_op | source)
XLA Modules:
  0.0 78.6 jit_solution(10708833330081688802)
XLA Ops:
  0.0 77.6 %shard_map.46 = bf16[4,4,8,32,128]{4,3,2,1,0:T(8,128)(2,1)S(1)} custom-call(bf16[4,2,2,8,64,128]{5,4,3,2,1,0:T(8,128)(2,1)} %bitcast.8, bf16[4,2,2,8,32,128]{5,4,3,2,1,0:T(8,128)(2,1)} %bitcast.9, bf16[4,4,2,2,8,32,128]{6,5,4,3,2,1,0:T(8,128)(2,1)} %bitcast.6, bf16[4,4,2,2,8,32,128]{6,5,4,3,2,1,0:T(8,128)(2,1)} %bitcast.7), custom_call_target="tpu_custom_call" | custom-call | tf_op jit(solution)/shard_map/pallas_call | solution.py:354
  77.6 1.0 %copy.6 = bf16[128,32,128]{2,1,0:T(8,128)(2,1)} copy(bf16[128,32,128]{2,1,0:T(8,128)(2,1)S(1)} %bitcast.5) | data formatting | bytes 2097152

commit v8 on v7

--- a/solution.py
+++ b/solution.py
@@ -151,7 +151,7 @@
         )
 
     near = [(i, h) for h in range(2) for i in (1, 3, 2, 0) if (i, h) != (0, 0)]
-    along_y = [2, 6, 4, 1, 3, 7, 5]
+    along_y = [4, 3, 5, 2, 6, 1, 7]
     along_z = [mate, (z + 2) % 4, (mate + 2) % 4]
 
     loads = [

time: 78.9 us -> 78.7 us (level)
  no operation moved by 1% of the time
where the time goes in v8:
time: 78.7 us; the launch traced here: 78.6 us
  Pallas kernels  77.6 us (99%)
  local copies, waits for them, and re-layouts  0.97 us (1%)
    pallas_call x1, Pallas kernels, local(): pl.pallas_call(kernel, out_shape=jax.ShapeDtypeStruct((4, 4, 8) + box, BF...  77.6 us

profile of v8, /device:TPU:4, one launch (start us, length us, event | category | flops | bytes accessed | tf_op | source)
XLA Modules:
  0.0 78.6 jit_solution(3974359504998482906)
XLA Ops:
  0.0 77.6 %shard_map.46 = bf16[4,4,8,32,128]{4,3,2,1,0:T(8,128)(2,1)S(1)} custom-call(bf16[4,2,2,8,64,128]{5,4,3,2,1,0:T(8,128)(2,1)} %bitcast.8, bf16[4,2,2,8,32,128]{5,4,3,2,1,0:T(8,128)(2,1)} %bitcast.9, bf16[4,4,2,2,8,32,128]{6,5,4,3,2,1,0:T(8,128)(2,1)} %bitcast.6, bf16[4,4,2,2,8,32,128]{6,5,4,3,2,1,0:T(8,128)(2,1)} %bitcast.7), custom_call_target="tpu_custom_call" | custom-call | tf_op jit(solution)/shard_map/pallas_call | solution.py:354
  77.6 1.0 %copy.6 = bf16[128,32,128]{2,1,0:T(8,128)(2,1)} copy(bf16[128,32,128]{2,1,0:T(8,128)(2,1)S(1)} %bitcast.5) | data formatting | bytes 2097152

commit v9 on v8

--- a/solution.py
+++ b/solution.py
@@ -180,7 +180,7 @@
     for i in range(1, 4):
         for to_z in (z, mate, z_of(a, 1 - z1)):
             peers.append(((x + i) % 4, to_z * 8 + yc))
-    for peer in peers:
+    for peer in peers[::-1]:
         pl.semaphore_signal(barrier, inc=1, device_id=peer, device_id_type=MESH)
 
     pl.semaphore_wait(barrier, len(peers))

time: 78.7 us -> 78.6 us (level)
  no operation moved by 1% of the time
where the time goes in v9:
time: 78.6 us; the launch traced here: 78.4 us
  Pallas kernels  77.5 us (99%)
  local copies, waits for them, and re-layouts  0.97 us (1%)
    pallas_call x1, Pallas kernels, local(): pl.pallas_call(kernel, out_shape=jax.ShapeDtypeStruct((4, 4, 8) + box, BF...  77.5 us

profile of v9, /device:TPU:4, one launch (start us, length us, event | category | flops | bytes accessed | tf_op | source)
XLA Modules:
  0.0 78.4 jit_solution(8309164096577313470)
XLA Ops:
  0.0 77.5 %shard_map.46 = bf16[4,4,8,32,128]{4,3,2,1,0:T(8,128)(2,1)S(1)} custom-call(bf16[4,2,2,8,64,128]{5,4,3,2,1,0:T(8,128)(2,1)} %bitcast.8, bf16[4,2,2,8,32,128]{5,4,3,2,1,0:T(8,128)(2,1)} %bitcast.9, bf16[4,4,2,2,8,32,128]{6,5,4,3,2,1,0:T(8,128)(2,1)} %bitcast.6, bf16[4,4,2,2,8,32,128]{6,5,4,3,2,1,0:T(8,128)(2,1)} %bitcast.7), custom_call_target="tpu_custom_call" | custom-call | tf_op jit(solution)/shard_map/pallas_call | solution.py:354
  77.5 1.0 %copy.6 = bf16[128,32,128]{2,1,0:T(8,128)(2,1)} copy(bf16[128,32,128]{2,1,0:T(8,128)(2,1)S(1)} %bitcast.5) | data formatting | bytes 2097152
